TPU v7x, 1024 devices: a whole 4x8x16 slice. The times are simulated.
1024 devices in a mesh: dp: 16 (over x_lo, y), seq: 64 (over z, x_hi, core).
Axes of the slice: x: 4 (x_hi: 2, x_lo: 2; x = x_hi * 2 + x_lo), y: 8, z: 16, core: 2. Of those that a mesh axis runs over, the one named last changes fastest.
Arguments:
- cotangent: bfloat16 [16, 64, 128, 1152], P('dp', None, 'seq'), may hold values from -6 to 6
- query_time: bfloat16 [16, 64, 128, 576], P('dp', None, 'seq'), may hold values from -6 to 6
- key_time: bfloat16 [16, 64, 128, 576], P('dp', None, 'seq'), may hold values from -6 to 6
- value_time: bfloat16 [16, 64, 128, 576], P('dp', None, 'seq'), may hold values from -6 to 6
- query_space: bfloat16 [16, 64, 128, 576], P('dp', 'seq'), may hold values from -6 to 6
- key_space: bfloat16 [16, 64, 128, 576], P('dp', 'seq'), may hold values from -6 to 6
- value_space: bfloat16 [16, 64, 128, 576], P('dp', 'seq'), may hold values from -6 to 6
- weight_time: bfloat16 [1152, 576], replicated, may hold values from -0.25 to 0.25
- weight_space: bfloat16 [1152, 576], replicated, may hold values from -0.25 to 0.25
- gate_time: float32 [16, 1152], P('dp'), may hold values from 0.25 to 2
- gate_space: float32 [16, 1152], P('dp'), may hold values from 0.25 to 2
Outputs:
- query_grad_time: bfloat16 [16, 64, 128, 576], P('dp', None, 'seq')
- key_grad_time: bfloat16 [16, 64, 128, 576], P('dp', None, 'seq')
- value_grad_time: bfloat16 [16, 64, 128, 576], P('dp', None, 'seq')
- query_grad_space: bfloat16 [16, 64, 128, 576], P('dp', 'seq')
- key_grad_space: bfloat16 [16, 64, 128, 576], P('dp', 'seq')
- value_grad_space: bfloat16 [16, 64, 128, 576], P('dp', 'seq')
- weight_grad_time: float32 [1152, 576], P('seq', 'dp')
- gate_grad_time: float32 [16, 1152], P('dp')
- gate_grad_space: float32 [16, 1152], P('dp')
All inputs are finite; a program needn't handle non-finite values.
Results may differ from a plain program's by a relative error of at most 0.035.
Values may be sent and summed in bfloat16 or wider, within the bound.
No kernel may reach another device: no remote copies, remote signals or barrier semaphores. Data moves between devices by JAX's collectives and lax.ppermute only.
A program may use at most 32 MiB of HBM per device.

v0:
```python
import functools
import math

import jax
import jax.numpy as jnp
import numpy as np
from jax import lax
from jax.experimental import pallas as pl
from jax.experimental.pallas import tpu as pltpu
from jax.sharding import Mesh
from jax.sharding import PartitionSpec as P

HD = 72
HEADS = 8
WIDTH = 576
MODEL = 1152
TOK = 128
NT = (((1,), (1,)), ((), ()))
TN = (((0,), (0,)), ((), ()))
NN = (((1,), (0,)), ((), ()))
F32 = jnp.float32
BF16 = jnp.bfloat16
DP = ("xl", "y")
SEQ = ("z", "xh", "c")
ROWS = ("z", "xh")
SCALE = 1.0 / math.sqrt(HD)


def dot(a, b, dims):
    return lax.dot_general(a, b, dims, preferred_element_type=F32)


def probs_of(key, query, keep):
    scores = dot(key, query, TN) * SCALE
    if keep is not None:
        scores = jnp.where(keep, scores, -jnp.inf)
    top = jnp.max(scores, axis=0, keepdims=True)
    e = jnp.exp(scores - top)
    return e / jnp.sum(e, axis=0, keepdims=True)


def same_position():
    i = lax.broadcasted_iota(jnp.int32, (TOK, TOK), 0)
    j = lax.broadcasted_iota(jnp.int32, (TOK, TOK), 1)
    return ((i + j) & 1) == 0


def turned(x):
    return x.astype(F32).T.astype(BF16)


def rows_of(ref, h):
    return ref[h * HD : (h + 1) * HD, :]


def forward_kernel(over_time, q_ref, k_ref, v_ref, out_ref, *turned_refs):
    keep = same_position() if over_time else None
    if over_time:
        for src, dst in zip((q_ref, k_ref, v_ref), turned_refs):
            dst[...] = turned(src[...])
        q_ref, k_ref, v_ref = turned_refs
    for h in range(HEADS):
        low = probs_of(rows_of(k_ref, h), rows_of(q_ref, h), keep).astype(BF16)
        out_ref[h * HD : (h + 1) * HD, :] = dot(rows_of(v_ref, h), low, NN).astype(BF16)


def project_kernel(cot_ref, gate_ref, w_ref, att_ref, d_ref, part_ref):
    cot = cot_ref[...].astype(F32)
    gated = (cot * gate_ref[...]).astype(BF16)
    d_ref[...] = dot(w_ref[...], gated, NT).astype(BF16)
    projected = dot(att_ref[...], w_ref[...], TN)
    part_ref[...] = jnp.sum(cot * projected, axis=0, keepdims=True)


def backward_kernel(over_time, q_ref, k_ref, v_ref, att_ref, d_ref, gq_ref, gk_ref, gv_ref, *scratch):
    keep = same_position() if over_time else None
    outs = scratch if over_time else (gq_ref, gk_ref, gv_ref)
    for h in range(HEADS):
        sl = slice(h * HD, (h + 1) * HD)
        q, k, v, a, d = (rows_of(r, h) for r in (q_ref, k_ref, v_ref, att_ref, d_ref))
        probs = probs_of(k, q, keep)
        low = probs.astype(BF16)
        d_probs = dot(v, d, TN)
        delta = jnp.sum(d.astype(F32) * a.astype(F32), axis=0, keepdims=True)
        d_scores = (probs * (d_probs - delta)).astype(BF16)
        grads = (dot(k, d_scores, NN) * SCALE, dot(q, d_scores, NT) * SCALE, dot(d, low, NT))
        for ref, g in zip(outs, grads):
            ref[sl, :] = g.astype(ref.dtype)
    if over_time:
        for src, dst in zip(scratch, (gq_ref, gk_ref, gv_ref)):
            dst[...] = src[...].T.astype(BF16)


def select_kernel(core_ref, own_ref, other_ref, gate_ref, out_ref):
    core = core_ref[0]
    row = lax.broadcasted_iota(jnp.int32, (WIDTH, 1), 0)
    block = (row * 3641) >> 16
    channel = row + 18 * (block + core)
    col = lax.broadcasted_iota(jnp.int32, (WIDTH, MODEL), 1)
    pick = jnp.where(col == channel, 1.0, 0.0).astype(BF16)
    for i, ref in enumerate((own_ref, other_ref)):
        gated = (ref[...].astype(F32) * gate_ref[...]).astype(BF16)
        out_ref[:, i * TOK : (i + 1) * TOK] = dot(pick, gated, NT).astype(BF16)


def product_kernel(norm, half_ref, own_ref, other_ref, sel_ref, keep_ref, send_ref):
    half = half_ref[0]
    sel = sel_ref[...]
    for ref, index in ((keep_ref, half), (send_ref, 1 - half)):
        rows = pl.ds(pl.multiple_of(index * 288, 32), 288)
        att = jnp.concatenate([own_ref[rows, :], other_ref[rows, :]], axis=1)
        ref[...] = (dot(att, sel, NT) * norm).astype(ref.dtype)


def join_kernel(keep_ref, came_ref, out_ref):
    total = (keep_ref[...] + came_ref[...].astype(F32)).astype(BF16)
    out_ref[...] = total.reshape(out_ref.shape)


def pack_kernel(core_ref, in_ref, time_ref, space_ref, came_ref, out_ref):
    total = jnp.sum(in_ref[...].astype(F32), axis=0)
    total = jnp.concatenate([total, jnp.zeros((4, WIDTH), F32)], axis=0)
    gate = jnp.where(core_ref[0] == 0, time_ref[...], space_ref[...]) + came_ref[...]
    last = gate[:, 1024:]
    tail = jnp.concatenate([last[:, 16 * a : 16 * a + 16] for a in range(8)], axis=0)
    gap = jnp.zeros((8, 22), F32)
    low = jnp.concatenate([gate[:, 128 * a : 128 * a + 128] for a in range(8)], axis=0)
    for m in range(32):
        parts = [total[8 * b : 8 * b + 8, 18 * m : 18 * m + 18] for b in range(5)]
        high = jnp.concatenate(parts + [gap, tail], axis=1)
        out_ref[m] = jnp.concatenate([high, low], axis=0).astype(BF16)


def finish_kernel(norm, in_ref, out_ref, gate_ref):
    total = jnp.sum(in_ref[...].astype(F32), axis=0)
    high = total[:8]
    flipped = high.T
    for b in range(5):
        n = 8 if b < 4 else 4
        out_ref[:, 8 * b : 8 * b + n] = flipped[18 * b : 18 * b + 18, :n]
    for a in range(8):
        gate_ref[:, 128 * a : 128 * a + 128] = total[8 + a : 9 + a, :] * norm
    last = jnp.concatenate([high[a : a + 1, 112:] for a in range(8)], axis=1)
    gate_ref[:, 1024:] = last * norm


def call(kernel, outs, *args, scratch=(), flops=0, scalars=0):
    specs = [pl.BlockSpec(memory_space=pltpu.SMEM)] * scalars
    specs += [pl.BlockSpec(memory_space=pltpu.VMEM)] * (len(args) - scalars)
    shapes = tuple(jax.ShapeDtypeStruct(s, d) for s, d in outs)
    return pl.pallas_call(
        kernel,
        out_shape=shapes,
        in_specs=specs,
        out_specs=tuple(pl.BlockSpec(memory_space=pltpu.VMEM) for _ in shapes),
        scratch_shapes=list(scratch),
        cost_estimate=pl.CostEstimate(flops=flops, bytes_accessed=1 << 20, transcendentals=0),
        compiler_params=pltpu.CompilerParams(vmem_limit_bytes=VMEM_LIMIT),
    )(*args)


def traded(x, axes):
    return lax.all_to_all(x, axes, 0, 0, tiled=True)


def partner(x, axis):
    return lax.ppermute(x, axis, [(0, 1), (1, 0)])


def swapped(x):
    return jnp.swapaxes(x[0, 0], 0, 1)


US = 400_000_000
VMEM_LIMIT = 16 << 20


def step(cot, qt, kt, vt, qs, ks, vs, wt, ws, gt, gs):
    norm_weight = 1.0 / math.sqrt(16 * 64 * 128)
    norm_gate = 1.0 / math.sqrt(64 * 128)
    col = ((WIDTH, TOK), BF16)
    core = lax.axis_index("c").astype(jnp.int32).reshape(1)
    half = lax.axis_index("xl").astype(jnp.int32).reshape(1)
    exchanged = traded(cot[0], SEQ)
    other_cot = partner(cot, "c")
    cot_t = cot.reshape(TOK, MODEL)
    wt_t = wt.T
    ws_t = ws.T
    q2, k2, v2 = (x.reshape(TOK, WIDTH) for x in (qt, kt, vt))
    att_t, q_t, k_t, v_t = call(functools.partial(forward_kernel, True), [col] * 4, q2, k2, v2, flops=4 * US)
    other_att = partner(att_t, "c")
    (selected,) = call(select_kernel, [((WIDTH, 2 * TOK), BF16)], core, cot_t, other_cot.reshape(TOK, MODEL), gt, scalars=1, flops=2 * US)
    block = (288, WIDTH)
    keep, send = call(functools.partial(product_kernel, norm_weight), [(block, F32), (block, BF16)], half, att_t, other_att, selected, scalars=1, flops=2 * US)
    came = partner(send, "xl")
    (terms,) = call(join_kernel, [((8, 36, WIDTH), BF16)], keep, came, flops=US)
    arrived = traded(terms, "y")
    part = ((1, MODEL), F32)
    d_t, part_t = call(project_kernel, [col, part], cot_t, gt, wt_t, att_t, flops=2 * US)
    q_s, k_s, v_s = (swapped(x) for x in (qs, ks, vs))
    (att_s,) = call(functools.partial(forward_kernel, False), [col], q_s, k_s, v_s, flops=3 * US)
    d_s, part_s = call(project_kernel, [col, part], exchanged.reshape(TOK, MODEL), gs, ws_t, att_s, flops=2 * US)
    came_gate = partner(jnp.where(core == 0, part_s, part_t), "c")
    (packed,) = call(pack_kernel, [((32, 16, 128), BF16)], core, arrived, part_t, part_s, came_gate, scalars=1, flops=US)
    rows = traded(packed, ROWS)
    tok = ((TOK, WIDTH), BF16)
    grads_t = call(functools.partial(backward_kernel, True), [tok] * 3, q_t, k_t, v_t, att_t, d_t, scratch=[pltpu.VMEM((WIDTH, TOK), F32)] * 3, flops=4 * US)
    grads_s = call(functools.partial(backward_kernel, False), [col] * 3, q_s, k_s, v_s, att_s, d_s, flops=4 * US)
    weight_grad, gate = call(functools.partial(finish_kernel, norm_gate), [((18, 36), F32), part], rows, flops=US)
    other_gate = partner(gate, "c")
    return (
        *(g.reshape(1, 64, 2, WIDTH) for g in grads_t),
        *(jnp.swapaxes(g, 0, 1)[None, None] for g in grads_s),
        weight_grad,
        jnp.where(core == 0, gate, other_gate),
        jnp.where(core == 0, other_gate, gate),
    )


def solution(mesh):
    fine = Mesh(np.array(mesh.devices).reshape(2, 8, 16, 2, 2), ("xl", "y", "z", "xh", "c"))
    by_pos = P(DP, None, SEQ, None)
    by_frame = P(DP, SEQ, None, None)
    in_specs = (by_pos,) * 4 + (by_frame,) * 3 + (P(), P(), P(DP, None), P(DP, None))
    out_specs = (by_pos,) * 3 + (by_frame,) * 3 + (P(SEQ, DP), P(DP, None), P(DP, None))
    return jax.shard_map(step, mesh=fine, in_specs=in_specs, out_specs=out_specs, check_vma=False)
```

profile of v0, /device:TPU:1, one launch (start us, length us, event | category | flops | bytes accessed | tf_op | source)
XLA Modules:
  0.0 108.4 jit_solution(13360486690279972795)
XLA Ops:
  0.6 0.0 copy-start.25
  0.7 23.4 %all-to-all-start = ((bf16[64,2,1152]{2,1,0:T(2,128)(2,1)}), bf16[64,2,1152]{2,1,0:T(2,128)(2,1)S(1)}, u32[]{:S(2)}, u32[]{:S(2)}) async-start(bf16[64,2,1152]{2,1,0:T(2,128)(2,1)} %bitcast.32), calls=%async_computation | async-start | bytes 589824 | tf_op jit(solution)/shard_map/all_to_all | solution.py:163
  24.1 2.4 %collective-permute-start.1 = (bf16[1,64,2,1152]{3,2,1,0:T(2,128)(2,1)}, bf16[1,64,2,1152]{3,2,1,0:T(2,128)(2,1)S(1)}, u32[]{:S(2)}, u32[]{:S(2)}) collective-permute-start(bf16[1,64,2,1152]{3,2,1,0:T(2,128)(2,1)} %param.11), channel_id=1, source_target_pairs={{0,1},{1,0},{2,3},{3,2},{4,5},{5,4},{6,7},{7,6},{8,9},{9,8},{10,11... | collective-permute-start | bytes 884744 | tf_op jit(solution)/shard_map/ppermute | solution.py:167
  26.4 1.0 reshape.54.q_ref
  27.5 1.0 reshape.55.k_ref
  28.5 0.1 reshape.56.v_ref
  28.7 0.0 copy-start.23
  28.7 0.0 copy-start.10
  28.7 1.0 shard_map.178
  29.8 0.0 copy-start.17
  29.8 0.7 copy-done.17
  30.4 0.7 copy-done.19
  31.1 0.7 copy-done.21
  31.8 2.0 %collective-permute-start = (bf16[576,128]{1,0:T(8,128)(2,1)S(1)}, bf16[576,128]{1,0:T(8,128)(2,1)S(1)}, u32[]{:S(2)}, u32[]{:S(2)}) collective-permute-start(bf16[576,128]{1,0:T(8,128)(2,1)S(1)} %get-tuple-element.30.att_ref.own_ref), channel_id=1, source_target_pairs={{0,1},{1,0},{2,3},{3,2},{4,5},{5,4},{6,7},{7,6},{8,9},{9,8},{10,11... | collective-permute-start | bytes 442376 | tf_op jit(solution)/shard_map/ppermute | solution.py:167
  33.7 0.0 copy-done.23
  33.7 0.1 reshape.57.cot_ref.own_ref
  33.9 0.0 collective-permute-done.1
  33.9 0.1 reshape.64.other_ref
  34.0 0.9 shard_map.184.sel_ref
  34.9 0.1 collective-permute-done.other_ref
  35.0 0.4 shard_map.185
  35.4 2.2 %collective-permute-start.2 = (bf16[288,576]{1,0:T(8,128)(2,1)S(1)}, bf16[288,576]{1,0:T(8,128)(2,1)S(1)}, u32[]{:S(2)}, u32[]{:S(2)}) collective-permute-start(bf16[288,576]{1,0:T(8,128)(2,1)S(1)} %get-tuple-element.40), channel_id=1, source_target_pairs={{0,512},{512,0},{1,513},{513,1},{2,514},{514,2},{3,515},{515,3},{4... | collective-permute-start | bytes 995336 | tf_op jit(solution)/shard_map/ppermute | solution.py:167
  37.7 0.0 copy-done.2
  37.7 0.0 copy-done.3
  37.7 0.0 copy-done.5
  37.7 0.9 shard_map.181.att_ref
  38.6 0.7 copy-done.12
  39.3 8.2 %collective-permute-done.2.came_ref = bf16[288,576]{1,0:T(8,128)(2,1)S(1)} collective-permute-done((bf16[288,576]{1,0:T(8,128)(2,1)S(1)}, bf16[288,576]{1,0:T(8,128)(2,1)S(1)}, u32[]{:S(2)}, u32[]{:S(2)}) %collective-permute-start.2) | collective-permute-done | bytes 331808 | tf_op jit(solution)/shard_map/ppermute | solution.py:167
  47.5 0.9 shard_map.186
  48.4 0.8 all-to-all-done
  49.2 6.8 %all-to-all-start.1 = ((bf16[8,36,576]{2,1,0:T(8,128)(2,1)}), bf16[8,36,576]{2,1,0:T(8,128)(2,1)S(1)}, u32[]{:S(2)}, u32[]{:S(2)}) async-start(bf16[8,36,576]{2,1,0:T(8,128)(2,1)} %shard_map.186), calls=%async_computation.1 | async-start | bytes 819200 | tf_op jit(solution)/shard_map/all_to_all | solution.py:163
  56.0 0.0 copy-start.8
  56.0 0.9 copy-done.8
  56.9 0.8 shard_map.179
  57.7 0.0 copy-start.15
  57.7 0.7 copy-done.15
  58.4 1.1 reshape.61.cot_ref
  59.5 0.9 copy-done.13
  60.4 0.8 shard_map.182
  61.2 0.0 copy-start.9
  61.2 0.0 copy-start.16
  61.2 0.0 copy-start.18
  61.2 0.0 copy-start.20
  61.2 0.0 copy-start.22
  61.3 2.6 %collective-permute-start.3 = (f32[1,1152]{1,0:T(1,128)S(1)}, f32[1,1152]{1,0:T(1,128)S(1)}, u32[]{:S(2)}, u32[]{:S(2)}) collective-permute-start(f32[1,1152]{1,0:T(1,128)S(1)} %broadcast_select_fusion.2), channel_id=1, source_target_pairs={{0,1},{1,0},{2,3},{3,2},{4,5},{5,4},{6,7},{7,6},{8,9},{9,8},{10,11... | collective-permute-start | bytes 13832 | tf_op jit(solution)/shard_map/ppermute | solution.py:167
  63.9 0.8 collective-permute-done.3.came_ref
  64.7 6.8 %all-to-all-done.1.in_ref = bf16[8,36,576]{2,1,0:T(8,128)(2,1)S(1)} async-done(((bf16[8,36,576]{2,1,0:T(8,128)(2,1)}), bf16[8,36,576]{2,1,0:T(8,128)(2,1)S(1)}, u32[]{:S(2)}, u32[]{:S(2)}) %all-to-all-start.1) | async-done | bytes 331808 | tf_op jit(solution)/shard_map/all_to_all | solution.py:163
  71.5 0.8 shard_map.187
  72.3 11.0 %all-to-all-start.2 = ((bf16[32,16,128]{2,1,0:T(8,128)(2,1)}), bf16[32,16,128]{2,1,0:T(8,128)(2,1)S(1)}, u32[]{:S(2)}, u32[]{:S(2)}) async-start(bf16[32,16,128]{2,1,0:T(8,128)(2,1)} %shard_map.187), calls=%async_computation.2 | async-start | bytes 262144 | tf_op jit(solution)/shard_map/all_to_all | solution.py:163
  83.4 2.3 %shard_map.180 = (bf16[128,576]{1,0:T(8,128)(2,1)S(1)}, bf16[128,576]{1,0:T(8,128)(2,1)S(1)}, bf16[128,576]{1,0:T(8,128)(2,1)S(1)}) custom-call(bf16[576,128]{1,0:T(8,128)(2,1)S(1)} %copy-done.18, bf16[576,128]{1,0:T(8,128)(2,1)S(1)} %copy-done.20, bf16[576,128]{1,0:T(8,128)(2,1)S(1)} %copy-done.22, bf16[576,128]{1,0:T(8,128)(2,1)S(1)} %copy-done.9, ...), custom_call_target="tpu_custom_call" | custom-call | flops 1600000000 | bytes 1048576 | tf_op jit(solution)/shard_map/pallas_call | solution.py:151
  85.7 0.0 copy-start.4
  85.7 0.0 copy-start.6
  85.7 0.7 reshape.58
  86.5 0.7 reshape.59
  87.2 0.7 reshape.60
  88.0 10.2 %all-to-all-done.2.in_ref = bf16[32,16,128]{2,1,0:T(8,128)(2,1)S(1)} async-done(((bf16[32,16,128]{2,1,0:T(8,128)(2,1)}), bf16[32,16,128]{2,1,0:T(8,128)(2,1)S(1)}, u32[]{:S(2)}, u32[]{:S(2)}) %all-to-all-start.2) | async-done | bytes 131104 | tf_op jit(solution)/shard_map/all_to_all | solution.py:163
  98.1 0.8 shard_map.188
  98.9 5.9 %collective-permute-start.4 = (f32[1,1152]{1,0:T(1,128)S(1)}, f32[1,1152]{1,0:T(1,128)S(1)}, u32[]{:S(2)}, u32[]{:S(2)}) collective-permute-start(f32[1,1152]{1,0:T(1,128)S(1)} %get-tuple-element.44), channel_id=1, source_target_pairs={{0,1},{1,0},{2,3},{3,2},{4,5},{5,4},{6,7},{7,6},{8,9},{9,8},{10,11... | collective-permute-start | bytes 13832 | tf_op jit(solution)/shard_map/ppermute | solution.py:167
  104.8 0.0 copy-done.4
  104.8 0.0 copy-done.6
  104.9 0.0 copy-done.14
  104.9 2.9 %shard_map.183 = (bf16[576,128]{1,0:T(8,128)(2,1)}, bf16[576,128]{1,0:T(8,128)(2,1)}, bf16[576,128]{1,0:T(8,128)(2,1)}) custom-call(bf16[576,128]{1,0:T(8,128)(2,1)S(1)} %bitcast.27, bf16[576,128]{1,0:T(8,128)(2,1)S(1)} %bitcast.29, bf16[576,128]{1,0:T(8,128)(2,1)S(1)} %bitcast.31, bf16[576,128]{1,0:T(8,128)(2,1)S(1)} %copy-done.14, ...), custom_call_target="tpu_custom_call" | custom-call | flops 1600000000 | bytes 1048576 | tf_op jit(solution)/shard_map/pallas_call | solution.py:151
  107.8 0.0 collective-permute-done.4
  107.8 0.6 broadcast_select_fusion
  (26 shorter events, 0.1 us)
Async XLA Ops:
  0.6 27.9 %copy-start.25 = (bf16[1,64,2,576]{3,2,1,0:T(2,128)(2,1)S(1)}, bf16[1,64,2,576]{3,2,1,0:T(2,128)(2,1)}, u32[]{:S(2)}) copy-start(bf16[1,64,2,576]{3,2,1,0:T(2,128)(2,1)} %param.14) | copy-start | bytes 442372
  0.7 48.5 %all-to-all-start = ((bf16[64,2,1152]{2,1,0:T(2,128)(2,1)}), bf16[64,2,1152]{2,1,0:T(2,128)(2,1)S(1)}, u32[]{:S(2)}, u32[]{:S(2)}) async-start(bf16[64,2,1152]{2,1,0:T(2,128)(2,1)} %bitcast.32), calls=%async_computation | async-start | bytes 589824 | tf_op jit(solution)/shard_map/all_to_all | solution.py:163
  24.1 9.8 %collective-permute-start.1 = (bf16[1,64,2,1152]{3,2,1,0:T(2,128)(2,1)}, bf16[1,64,2,1152]{3,2,1,0:T(2,128)(2,1)S(1)}, u32[]{:S(2)}, u32[]{:S(2)}) collective-permute-start(bf16[1,64,2,1152]{3,2,1,0:T(2,128)(2,1)} %param.11), channel_id=1, source_target_pairs={{0,1},{1,0},{2,3},{3,2},{4,5},{5,4},{6,7},{7,6},{8,9},{9,8},{10,11... | collective-permute-start | bytes 884744 | tf_op jit(solution)/shard_map/ppermute | solution.py:167
  28.7 5.0 %copy-start.23 = (bf16[1,64,2,1152]{3,2,1,0:T(2,128)(2,1)S(1)}, bf16[1,64,2,1152]{3,2,1,0:T(2,128)(2,1)}, u32[]{:S(2)}) copy-start(bf16[1,64,2,1152]{3,2,1,0:T(2,128)(2,1)} %param.11) | copy-start | bytes 884740
  28.7 5.3 %copy-start.10 = (f32[1,1152]{1,0:T(1,128)S(1)}, f32[1,1152]{1,0:T(1,128)}, u32[]{:S(2)}) copy-start(f32[1,1152]{1,0:T(1,128)} %gate_ref.5) | copy-start | bytes 13828
  29.8 0.7 copy-start.17
  30.4 0.7 copy-start.19
  31.1 0.7 copy-start.21
  31.7 3.3 %copy-start.7 = (bf16[576,128]{1,0:T(8,128)(2,1)}, bf16[576,128]{1,0:T(8,128)(2,1)S(1)}, u32[]{:S(2)}) copy-start(bf16[576,128]{1,0:T(8,128)(2,1)S(1)} %get-tuple-element.30.att_ref.own_ref) | copy-start | bytes 442372
  31.8 3.3 %collective-permute-start = (bf16[576,128]{1,0:T(8,128)(2,1)S(1)}, bf16[576,128]{1,0:T(8,128)(2,1)S(1)}, u32[]{:S(2)}, u32[]{:S(2)}) collective-permute-start(bf16[576,128]{1,0:T(8,128)(2,1)S(1)} %get-tuple-element.30.att_ref.own_ref), channel_id=1, source_target_pairs={{0,1},{1,0},{2,3},{3,2},{4,5},{5,4},{6,7},{7,6},{8,9},{9,8},{10,11... | collective-permute-start | bytes 442376 | tf_op jit(solution)/shard_map/ppermute | solution.py:167
  35.0 2.7 %copy-start.2 = (bf16[1,1,128,576]{2,3,1,0:T(8,128)(2,1)S(1)}, bf16[1,1,128,576]{2,3,1,0:T(8,128)(2,1)}, u32[]{:S(2)}) copy-start(bf16[1,1,128,576]{2,3,1,0:T(8,128)(2,1)} %param.15) | copy-start | bytes 442372
  35.0 2.7 %copy-start.3 = (bf16[1,1,128,576]{2,3,1,0:T(8,128)(2,1)S(1)}, bf16[1,1,128,576]{2,3,1,0:T(8,128)(2,1)}, u32[]{:S(2)}) copy-start(bf16[1,1,128,576]{2,3,1,0:T(8,128)(2,1)} %param.16) | copy-start | bytes 442372
  35.0 2.7 %copy-start.5 = (bf16[1,1,128,576]{2,3,1,0:T(8,128)(2,1)S(1)}, bf16[1,1,128,576]{2,3,1,0:T(8,128)(2,1)}, u32[]{:S(2)}) copy-start(bf16[1,1,128,576]{2,3,1,0:T(8,128)(2,1)} %param.17) | copy-start | bytes 442372
  35.4 12.1 %collective-permute-start.2 = (bf16[288,576]{1,0:T(8,128)(2,1)S(1)}, bf16[288,576]{1,0:T(8,128)(2,1)S(1)}, u32[]{:S(2)}, u32[]{:S(2)}) collective-permute-start(bf16[288,576]{1,0:T(8,128)(2,1)S(1)} %get-tuple-element.40), channel_id=1, source_target_pairs={{0,512},{512,0},{1,513},{513,1},{2,514},{514,2},{3,515},{515,3},{4... | collective-permute-start | bytes 995336 | tf_op jit(solution)/shard_map/ppermute | solution.py:167
  38.6 0.7 copy-start.12
  39.3 16.7 %copy-start = (bf16[1152,576]{0,1:T(8,128)(2,1)S(1)}, bf16[1152,576]{0,1:T(8,128)(2,1)}, u32[]{:S(2)}) copy-start(bf16[1152,576]{0,1:T(8,128)(2,1)} %param.18) | copy-start | bytes 3981316
  49.2 6.8 %copy-start.24 = (bf16[64,2,1152]{2,1,0:T(2,128)(2,1)}, bf16[64,2,1152]{2,1,0:T(2,128)(2,1)S(1)}, u32[]{:S(2)}) copy-start(bf16[64,2,1152]{2,1,0:T(2,128)(2,1)S(1)} %all-to-all-done) | copy-start | bytes 884740
  49.2 22.3 %all-to-all-start.1 = ((bf16[8,36,576]{2,1,0:T(8,128)(2,1)}), bf16[8,36,576]{2,1,0:T(8,128)(2,1)S(1)}, u32[]{:S(2)}, u32[]{:S(2)}) async-start(bf16[8,36,576]{2,1,0:T(8,128)(2,1)} %shard_map.186), calls=%async_computation.1 | async-start | bytes 819200 | tf_op jit(solution)/shard_map/all_to_all | solution.py:163
  56.0 0.9 copy-start.8
  56.9 2.5 %copy-start.1 = (bf16[1152,576]{0,1:T(8,128)(2,1)S(1)}, bf16[1152,576]{0,1:T(8,128)(2,1)}, u32[]{:S(2)}) copy-start(bf16[1152,576]{0,1:T(8,128)(2,1)} %param.19) | copy-start | bytes 3981316
  56.9 2.5 %copy-start.11 = (f32[1,1152]{1,0:T(1,128)S(1)}, f32[1,1152]{1,0:T(1,128)}, u32[]{:S(2)}) copy-start(f32[1,1152]{1,0:T(1,128)} %gate_ref.4) | copy-start | bytes 13828
  57.7 0.7 copy-start.15
  59.5 0.9 copy-start.13
  61.2 22.2 %copy-start.9 = (bf16[576,128]{1,0:T(8,128)(2,1)S(1)}, bf16[576,128]{1,0:T(8,128)(2,1)}, u32[]{:S(2)}) copy-start(bf16[576,128]{1,0:T(8,128)(2,1)} %copy-done.7) | copy-start | bytes 442372
  61.2 22.2 %copy-start.16 = (bf16[576,128]{1,0:T(8,128)(2,1)S(1)}, bf16[576,128]{1,0:T(8,128)(2,1)}, u32[]{:S(2)}) copy-start(bf16[576,128]{1,0:T(8,128)(2,1)} %copy-done.15) | copy-start | bytes 442372
  61.2 22.2 %copy-start.18 = (bf16[576,128]{1,0:T(8,128)(2,1)S(1)}, bf16[576,128]{1,0:T(8,128)(2,1)}, u32[]{:S(2)}) copy-start(bf16[576,128]{1,0:T(8,128)(2,1)} %copy-done.17) | copy-start | bytes 442372
  61.2 22.2 %copy-start.20 = (bf16[576,128]{1,0:T(8,128)(2,1)S(1)}, bf16[576,128]{1,0:T(8,128)(2,1)}, u32[]{:S(2)}) copy-start(bf16[576,128]{1,0:T(8,128)(2,1)} %copy-done.19) | copy-start | bytes 442372
  61.2 22.2 %copy-start.22 = (bf16[576,128]{1,0:T(8,128)(2,1)S(1)}, bf16[576,128]{1,0:T(8,128)(2,1)}, u32[]{:S(2)}) copy-start(bf16[576,128]{1,0:T(8,128)(2,1)} %copy-done.21) | copy-start | bytes 442372
  61.3 3.4 %collective-permute-start.3 = (f32[1,1152]{1,0:T(1,128)S(1)}, f32[1,1152]{1,0:T(1,128)S(1)}, u32[]{:S(2)}, u32[]{:S(2)}) collective-permute-start(f32[1,1152]{1,0:T(1,128)S(1)} %broadcast_select_fusion.2), channel_id=1, source_target_pairs={{0,1},{1,0},{2,3},{3,2},{4,5},{5,4},{6,7},{7,6},{8,9},{9,8},{10,11... | collective-permute-start | bytes 13832 | tf_op jit(solution)/shard_map/ppermute | solution.py:167
  72.3 25.8 %all-to-all-start.2 = ((bf16[32,16,128]{2,1,0:T(8,128)(2,1)}), bf16[32,16,128]{2,1,0:T(8,128)(2,1)S(1)}, u32[]{:S(2)}, u32[]{:S(2)}) async-start(bf16[32,16,128]{2,1,0:T(8,128)(2,1)} %shard_map.187), calls=%async_computation.2 | async-start | bytes 262144 | tf_op jit(solution)/shard_map/all_to_all | solution.py:163
  85.7 19.1 %copy-start.4 = (bf16[1,1,128,576]{2,3,1,0:T(8,128)(2,1)S(1)}, bf16[1,1,128,576]{2,3,1,0:T(8,128)(2,1)}, u32[]{:S(2)}) copy-start(bf16[1,1,128,576]{2,3,1,0:T(8,128)(2,1)} %param.16) | copy-start | bytes 442372
  85.7 19.1 %copy-start.6 = (bf16[1,1,128,576]{2,3,1,0:T(8,128)(2,1)S(1)}, bf16[1,1,128,576]{2,3,1,0:T(8,128)(2,1)}, u32[]{:S(2)}) copy-start(bf16[1,1,128,576]{2,3,1,0:T(8,128)(2,1)} %param.17) | copy-start | bytes 442372
  85.7 19.1 %copy-start.14 = (bf16[576,128]{1,0:T(8,128)(2,1)S(1)}, bf16[576,128]{1,0:T(8,128)(2,1)}, u32[]{:S(2)}) copy-start(bf16[576,128]{1,0:T(8,128)(2,1)} %copy-done.12) | copy-start | bytes 442372
  98.9 8.9 %collective-permute-start.4 = (f32[1,1152]{1,0:T(1,128)S(1)}, f32[1,1152]{1,0:T(1,128)S(1)}, u32[]{:S(2)}, u32[]{:S(2)}) collective-permute-start(f32[1,1152]{1,0:T(1,128)S(1)} %get-tuple-element.44), channel_id=1, source_target_pairs={{0,1},{1,0},{2,3},{3,2},{4,5},{5,4},{6,7},{7,6},{8,9},{9,8},{10,11... | collective-permute-start | bytes 13832 | tf_op jit(solution)/shard_map/ppermute | solution.py:167
where the time goes:
time: 109 us; the launch traced here: 108 us
  starting transfers between devices  56.3 us (52%)
  waiting for transfers between devices  26.9 us (25%)
  Pallas kernels  12.5 us (11%)
  local copies, waits for them, and re-layouts  10.9 us (10%)
    all_to_all x3, starting transfers between devices, traded(): return lax.all_to_all(x, axes, 0, 0, tiled=True)  41.2 us
    all_to_all x3, waiting for transfers between devices, traded(): return lax.all_to_all(x, axes, 0, 0, tiled=True)  17.8 us
    ppermute x5, starting transfers between devices, partner(): return lax.ppermute(x, axis, [(0, 1), (1, 0)])  15.1 us
    pallas_call x11, Pallas kernels, call(): pl.pallas_call(kernel, out_shape=shapes, in_specs=specs, out_specs=tuple(...  12.5 us
    ppermute x5, waiting for transfers between devices, partner(): return lax.ppermute(x, axis, [(0, 1), (1, 0)])  9.14 us
    unnamed x52, local copies, waits for them, and re-layouts  5.21 us
    reshape x3, local copies, waits for them, and re-layouts, step(): q2, k2, v2 = (x.reshape(TOK, WIDTH) for x in (qt, kt, vt))  2.22 us
    reshape x3, local copies, waits for them, and re-layouts, step(): g.reshape(1, 64, 2, WIDTH)  2.21 us
  transfers between devices with their start and end apart: 8, of which 6 were waited for; matrix products, arithmetic and copies ran while one was open for 5% of the time, Pallas kernels for 10%

commit v1 on v0

v1 whole, which is shorter than its diff:
```python
import functools
import math

import jax
import jax.numpy as jnp
import numpy as np
from jax import lax
from jax.experimental import pallas as pl
from jax.experimental.pallas import tpu as pltpu
from jax.sharding import Mesh
from jax.sharding import PartitionSpec as P

HD = 72
HEADS = 8
WIDTH = 576
MODEL = 1152
TOK = 128
NT = (((1,), (1,)), ((), ()))
TN = (((0,), (0,)), ((), ()))
NN = (((1,), (0,)), ((), ()))
F32 = jnp.float32
BF16 = jnp.bfloat16
DP = ("xl", "y")
SEQ = ("z", "xh", "c")
ROWS = ("z", "xh")
SCALE = 1.0 / math.sqrt(HD)


def dot(a, b, dims):
    return lax.dot_general(a, b, dims, preferred_element_type=F32)


def probs_of(key, query, keep):
    scores = dot(key, query, TN) * SCALE
    if keep is not None:
        scores = jnp.where(keep, scores, -jnp.inf)
    top = jnp.max(scores, axis=0, keepdims=True)
    e = jnp.exp(scores - top)
    return e / jnp.sum(e, axis=0, keepdims=True)


def same_position():
    i = lax.broadcasted_iota(jnp.int32, (TOK, TOK), 0)
    j = lax.broadcasted_iota(jnp.int32, (TOK, TOK), 1)
    return ((i + j) & 1) == 0


def turned(x):
    return x.astype(F32).T.astype(BF16)


def rows_of(ref, h):
    return ref[h * HD : (h + 1) * HD, :]


def forward_kernel(q_ref, k_ref, v_ref, out_ref):
    for h in range(HEADS):
        low = probs_of(rows_of(k_ref, h), rows_of(q_ref, h), None).astype(BF16)
        out_ref[h * HD : (h + 1) * HD, :] = dot(rows_of(v_ref, h), low, NN).astype(BF16)


def flat(ref):
    x = ref[...]
    return x.reshape(TOK, x.shape[-1])


def picked(core, gated):
    row = lax.broadcasted_iota(jnp.int32, (WIDTH, 1), 0)
    block = (row * 3641) >> 16
    channel = row + 18 * (block + core)
    col = lax.broadcasted_iota(jnp.int32, (WIDTH, MODEL), 1)
    pick = jnp.where(col == channel, 1.0, 0.0).astype(BF16)
    return dot(pick, gated, NT).astype(BF16)


def start_kernel(core_ref, gate_ref, *rest):
    sources, (send_ref, own_ref), landed, (q_t, k_t, v_t, sems) = rest[:4], rest[4:6], rest[6:10], rest[10:]
    copies = [pltpu.make_async_copy(a, b, sems.at[i]) for i, (a, b) in enumerate(zip(sources, landed))]
    for copy in copies:
        copy.start()
    keep = same_position()
    for copy in copies:
        copy.wait()
    q_ref, k_ref, v_ref, cot_ref = landed
    for src, dst in zip((q_ref, k_ref, v_ref), (q_t, k_t, v_t)):
        dst[...] = turned(flat(src))
    for h in range(HEADS):
        low = probs_of(rows_of(k_t, h), rows_of(q_t, h), keep).astype(BF16)
        send_ref[h * HD : (h + 1) * HD, :] = dot(rows_of(v_t, h), low, NN).astype(BF16)
    gated = (flat(cot_ref).astype(F32) * gate_ref[...]).astype(BF16)
    core = core_ref[0]
    own_ref[...] = picked(core, gated)
    send_ref[WIDTH:, :] = picked(1 - core, gated)


def project_kernel(cot_ref, gate_ref, w_ref, att_ref, d_ref, part_ref):
    cot = flat(cot_ref).astype(F32)
    gated = (cot * gate_ref[...]).astype(BF16)
    d_ref[...] = dot(w_ref[...], gated, NT).astype(BF16)
    projected = dot(att_ref[:WIDTH, :], w_ref[...], TN)
    part_ref[...] = jnp.sum(cot * projected, axis=0, keepdims=True)


def backward_kernel(over_time, q_ref, k_ref, v_ref, att_ref, d_ref, gq_ref, gk_ref, gv_ref, *scratch):
    keep = same_position() if over_time else None
    outs = (gq_ref, gk_ref, gv_ref)
    if over_time:
        for src, dst in zip((q_ref, k_ref, v_ref), scratch):
            dst[...] = turned(flat(src))
        q_ref, k_ref, v_ref = scratch[:3]
        outs = scratch[3:]
    for h in range(HEADS):
        sl = slice(h * HD, (h + 1) * HD)
        q, k, v, a, d = (rows_of(r, h) for r in (q_ref, k_ref, v_ref, att_ref, d_ref))
        probs = probs_of(k, q, keep)
        low = probs.astype(BF16)
        d_probs = dot(v, d, TN)
        delta = jnp.sum(d.astype(F32) * a.astype(F32), axis=0, keepdims=True)
        d_scores = (probs * (d_probs - delta)).astype(BF16)
        grads = (dot(k, d_scores, NN) * SCALE, dot(q, d_scores, NT) * SCALE, dot(d, low, NT))
        for ref, g in zip(outs, grads):
            ref[sl, :] = g.astype(ref.dtype)
    if over_time:
        for src, dst in zip(outs, (gq_ref, gk_ref, gv_ref)):
            dst[...] = src[...].T.astype(BF16).reshape(dst.shape)


def product_kernel(norm, y_ref, mine_ref, own_ref, came_ref, keep_ref, *rest):
    sends, total = rest[:7], rest[7]
    terms = dot(mine_ref[:WIDTH, :], own_ref[...], NT) + dot(came_ref[:WIDTH, :], came_ref[WIDTH:, :], NT)
    terms = terms * norm
    for i in range(16):
        total[40 * i : 40 * i + 36, :] = terms[36 * i : 36 * i + 36, :]
    y = y_ref[0]

    def block(at):
        at = jnp.where(at >= 8, at - 8, at)
        parts = [total[pl.ds(pl.multiple_of(320 * x + 40 * at, 8), 40), :][:36] for x in (0, 1)]
        return jnp.concatenate(parts, axis=0)

    keep_ref[...] = block(y)
    for shift, ref in enumerate(sends, 1):
        ref[...] = block(y + shift).astype(BF16)


def gather_kernel(half_ref, keep_ref, *rest):
    came, (own_ref, send_ref) = rest[:7], rest[7:]
    total = keep_ref[...]
    for ref in came:
        total = total + ref[...].astype(F32)
    first = half_ref[0] == 0
    low, high = total[:36], total[36:]
    own_ref[...] = jnp.where(first, low, high)
    send_ref[...] = jnp.where(first, high, low).astype(BF16)


def pack_kernel(core_ref, own_ref, in_ref, time_ref, space_ref, came_ref, out_ref):
    total = own_ref[...] + in_ref[...].astype(F32)
    total = jnp.concatenate([total, jnp.zeros((4, WIDTH), F32)], axis=0)
    gate = jnp.where(core_ref[0] == 0, time_ref[...], space_ref[...]) + came_ref[...]
    last = gate[:, 1024:]
    tail = jnp.concatenate([last[:, 16 * a : 16 * a + 16] for a in range(8)], axis=0)
    gap = jnp.zeros((8, 22), F32)
    low = jnp.concatenate([gate[:, 128 * a : 128 * a + 128] for a in range(8)], axis=0)
    for m in range(32):
        parts = [total[8 * b : 8 * b + 8, 18 * m : 18 * m + 18] for b in range(5)]
        high = jnp.concatenate(parts + [gap, tail], axis=1)
        out_ref[m] = jnp.concatenate([high, low], axis=0).astype(BF16)


def finish_kernel(norm, in_ref, out_ref, gate_ref):
    total = jnp.sum(in_ref[...].astype(F32), axis=0)
    high = total[:8]
    flipped = high.T
    for b in range(5):
        n = 8 if b < 4 else 4
        out_ref[:, 8 * b : 8 * b + n] = flipped[18 * b : 18 * b + 18, :n]
    for a in range(8):
        gate_ref[:, 128 * a : 128 * a + 128] = total[8 + a : 9 + a, :] * norm
    last = jnp.concatenate([high[a : a + 1, 112:] for a in range(8)], axis=1)
    gate_ref[:, 1024:] = last * norm


US = 400_000_000
VMEM_LIMIT = 16 << 20
FULL = 66_000_000


def call(kernel, outs, *args, scratch=(), flops=0, scalars=0, far=0, vmem=VMEM_LIMIT):
    specs = [pl.BlockSpec(memory_space=pltpu.SMEM)] * scalars
    specs += [pl.BlockSpec(memory_space=pltpu.VMEM)] * (len(args) - scalars - far)
    specs += [pl.BlockSpec(memory_space=pltpu.HBM)] * far
    shapes = tuple(jax.ShapeDtypeStruct(s, d) for s, d in outs)
    return pl.pallas_call(
        kernel,
        out_shape=shapes,
        in_specs=specs,
        out_specs=tuple(pl.BlockSpec(memory_space=pltpu.VMEM) for _ in shapes),
        scratch_shapes=list(scratch),
        cost_estimate=pl.CostEstimate(flops=flops, bytes_accessed=1 << 20, transcendentals=0),
        compiler_params=pltpu.CompilerParams(vmem_limit_bytes=vmem),
    )(*args)


def traded(x, axes):
    return lax.all_to_all(x, axes, 0, 0, tiled=True)


def partner(x, axis):
    return lax.ppermute(x, axis, [(0, 1), (1, 0)])


def shifted(x, axis, step, size):
    return lax.ppermute(x, axis, [(i, (i + step) % size) for i in range(size)])


def swapped(x):
    return jnp.swapaxes(x[0, 0], 0, 1)


def step(cot, qt, kt, vt, qs, ks, vs, wt, ws, gt, gs):
    norm_weight = 1.0 / math.sqrt(16 * 64 * 128)
    norm_gate = 1.0 / math.sqrt(64 * 128)
    col = ((WIDTH, TOK), BF16)
    core = lax.axis_index("c").astype(jnp.int32).reshape(1)
    half = lax.axis_index("xl").astype(jnp.int32).reshape(1)
    place = lax.axis_index("y").astype(jnp.int32).reshape(1)
    exchanged = traded(cot[0], SEQ)
    cot_t = cot[0]
    wt_t = wt.T
    ws_t = ws.T
    time_in = (qt[0], kt[0], vt[0])
    turned_in = [pltpu.VMEM((WIDTH, TOK), BF16)] * 3
    landing = [pltpu.VMEM(x.shape, BF16) for x in (*time_in, cot_t)]
    mine, own_rows = call(start_kernel, [((2 * WIDTH, TOK), BF16), col], core, gt, *time_in, cot_t, scratch=landing + turned_in + [pltpu.SemaphoreType.DMA((4,))], scalars=1, far=4, vmem=FULL, flops=4 * US)
    came = partner(mine, "c")
    block = (72, WIDTH)
    keep, *sends = call(functools.partial(product_kernel, norm_weight), [(block, F32)] + [(block, BF16)] * 7, place, mine, own_rows, came, scratch=[pltpu.VMEM((640, WIDTH), F32)], scalars=1, flops=2 * US)
    blocks = [shifted(x, "y", k, 8) for k, x in enumerate(sends, 1)]
    part_rows = (36, WIDTH)
    own_half, send_half = call(gather_kernel, [(part_rows, F32), (part_rows, BF16)], half, keep, *blocks, scalars=1, flops=US)
    came_half = partner(send_half, "xl")
    part = ((1, MODEL), F32)
    d_t, part_t = call(project_kernel, [col, part], cot_t, gt, wt_t, mine, flops=2 * US)
    q_s, k_s, v_s = (swapped(x) for x in (qs, ks, vs))
    (att_s,) = call(forward_kernel, [col], q_s, k_s, v_s, flops=3 * US)
    d_s, part_s = call(project_kernel, [col, part], exchanged, gs, ws_t, att_s, flops=2 * US)
    came_gate = partner(jnp.where(core == 0, part_s, part_t), "c")
    (packed,) = call(pack_kernel, [((32, 16, 128), BF16)], core, own_half, came_half, part_t, part_s, came_gate, scalars=1, flops=US)
    rows = traded(packed, ROWS)
    tok = ((64, 2, WIDTH), BF16)
    grads_t = call(functools.partial(backward_kernel, True), [tok] * 3, *time_in, mine, d_t, scratch=turned_in + [pltpu.VMEM((WIDTH, TOK), F32)] * 3, flops=4 * US)
    grads_s = call(functools.partial(backward_kernel, False), [col] * 3, q_s, k_s, v_s, att_s, d_s, flops=4 * US)
    weight_grad, gate = call(functools.partial(finish_kernel, norm_gate), [((18, 36), F32), part], rows, flops=US)
    other_gate = partner(gate, "c")
    return (
        *(g[None] for g in grads_t),
        *(jnp.swapaxes(g, 0, 1)[None, None] for g in grads_s),
        weight_grad,
        jnp.where(core == 0, gate, other_gate),
        jnp.where(core == 0, other_gate, gate),
    )


def solution(mesh):
    fine = Mesh(np.array(mesh.devices).reshape(2, 8, 16, 2, 2), ("xl", "y", "z", "xh", "c"))
    by_pos = P(DP, None, SEQ, None)
    by_frame = P(DP, SEQ, None, None)
    in_specs = (by_pos,) * 4 + (by_frame,) * 3 + (P(), P(), P(DP, None), P(DP, None))
    out_specs = (by_pos,) * 3 + (by_frame,) * 3 + (P(SEQ, DP), P(DP, None), P(DP, None))
    return jax.shard_map(step, mesh=fine, in_specs=in_specs, out_specs=out_specs, check_vma=False)
```

time: 109 us -> 120 us (1.10)
  starting transfers between devices: 56.3 us -> 79.4 us
  waiting for transfers between devices: 26.9 us -> 18 us
  local copies, waits for them, and re-layouts: 10.9 us -> 3.29 us
  Pallas kernels: 12.5 us -> 17.2 us
    ppermute x0 -> x7, starting transfers between devices: none -> 28.4 us  [shifted(): return lax.ppermute(x, axis, [(i, (i + step) % size) for i in range(size)])]
    ppermute x5 -> x4, waiting for transfers between devices: 9.14 us -> 2.19 us  [partner(): return lax.ppermute(x, axis, [(0, 1), (1, 0)])]
    all_to_all x3 -> x2, waiting for transfers between devices: 17.8 us -> 11.9 us  [traded(): return lax.all_to_all(x, axes, 0, 0, tiled=True)]
    reshape x9 -> x0, local copies, waits for them, and re-layouts: 5.73 us -> none  [the longest x3 2.22 us: step(): q2, k2, v2 = (x.reshape(TOK, WIDTH) for x in (qt, kt, vt))]
    pallas_call x11 -> x10, Pallas kernels: 12.5 us -> 17.2 us  [call(): pl.pallas_call(kernel, out_shape=shapes, in_specs=specs, out_specs=tuple(...]
    ppermute x0 -> x7, waiting for transfers between devices: none -> 3.88 us  [shifted(): return lax.ppermute(x, axis, [(i, (i + step) % size) for i in range(size)])]
    all_to_all x3 -> x2, starting transfers between devices: 41.2 us -> 38.1 us  [traded(): return lax.all_to_all(x, axes, 0, 0, tiled=True)]
    ppermute x5 -> x4, starting transfers between devices: 15.1 us -> 12.9 us  [partner(): return lax.ppermute(x, axis, [(0, 1), (1, 0)])]
  transfers between devices with their start and end apart: 8 -> 13, of which waited for: 6 -> 5; matrix products, arithmetic and copies ran while one was open for 5% -> 0% of each run, Pallas kernels for 10% -> 13%
where the time goes in v1:
time: 120 us
  starting transfers between devices  79.4 us (66%)
  waiting for transfers between devices  18 us (15%)
  Pallas kernels  17.2 us (14%)
  local copies, waits for them, and re-layouts  3.29 us (3%)
    all_to_all x2, starting transfers between devices, traded(): return lax.all_to_all(x, axes, 0, 0, tiled=True)  38.1 us
    ppermute x7, starting transfers between devices, shifted(): return lax.ppermute(x, axis, [(i, (i + step) % size) for i in range(size)])  28.4 us
    pallas_call x10, Pallas kernels, call(): pl.pallas_call(kernel, out_shape=shapes, in_specs=specs, out_specs=tuple(...  17.2 us
    ppermute x4, starting transfers between devices, partner(): return lax.ppermute(x, axis, [(0, 1), (1, 0)])  12.9 us
    all_to_all x2, waiting for transfers between devices, traded(): return lax.all_to_all(x, axes, 0, 0, tiled=True)  11.9 us
    ppermute x7, waiting for transfers between devices, shifted(): return lax.ppermute(x, axis, [(i, (i + step) % size) for i in range(size)])  3.88 us
    unnamed x42, local copies, waits for them, and re-layouts  3.29 us
  transfers between devices with their start and end apart: 13, of which 5 were waited for; matrix products, arithmetic and copies ran while one was open for 0% of the time, Pallas kernels for 13%

profile of v1, /device:TPU:1, one launch (start us, length us, event | category | flops | bytes accessed | tf_op | source)
XLA Modules:
  0.0 119.6 jit_solution(9650936623612085154)
XLA Ops:
  0.6 23.3 %all-to-all-start = ((bf16[64,2,1152]{2,1,0:T(2,128)(2,1)}), bf16[64,2,1152]{2,1,0:T(2,128)(2,1)S(1)}, u32[]{:S(2)}, u32[]{:S(2)}) async-start(bf16[64,2,1152]{2,1,0:T(2,128)(2,1)} %bitcast.31), calls=%async_computation | async-start | bytes 589824 | tf_op jit(solution)/shard_map/all_to_all | solution.py:206
  23.9 4.5 %shard_map.178 = (bf16[1152,128]{1,0:T(8,128)(2,1)}, bf16[576,128]{1,0:T(8,128)(2,1)}) custom-call(s32[1]{0:T(128)} %bitcast.3.core_ref, f32[1,1152]{1,0:T(1,128)} %gate_ref.4, bf16[64,2,576]{2,1,0:T(2,128)(2,1)} %bitcast.36, bf16[64,2,576]{2,1,0:T(2,128)(2,1)} %bitcast.38, bf16[64,2,576]{2,1,0:T(2,128)(2,1)} %bitcast.40, bf16[64,2,1152]{2,1,0:T(2,128)(2,1)} %bitcast.32), custom_call_target="tpu_custom_call" | custom-call | flops 1600000000 | bytes 1048576 | tf_op jit(solution)/shard_map/pallas_call | solution.py:194
  28.4 2.4 %collective-permute-start = (bf16[1152,128]{1,0:T(8,128)(2,1)}, bf16[1152,128]{1,0:T(8,128)(2,1)S(1)}, u32[]{:S(2)}, u32[]{:S(2)}) collective-permute-start(bf16[1152,128]{1,0:T(8,128)(2,1)} %get-tuple-element.33.att_ref.mine_ref), channel_id=1, source_target_pairs={{0,1},{1,0},{2,3},{3,2},{4,5},{5,4},{6,7},{7,6},{8,9},{9,8},{10,11... | collective-permute-start | bytes 884744 | tf_op jit(solution)/shard_map/ppermute | solution.py:210
  30.8 1.4 %collective-permute-done.came_ref = bf16[1152,128]{1,0:T(8,128)(2,1)S(1)} collective-permute-done((bf16[1152,128]{1,0:T(8,128)(2,1)}, bf16[1152,128]{1,0:T(8,128)(2,1)S(1)}, u32[]{:S(2)}, u32[]{:S(2)}) %collective-permute-start) | collective-permute-done | bytes 294944 | tf_op jit(solution)/shard_map/ppermute | solution.py:210
  32.2 1.0 copy-done.3
  33.2 0.9 copy-done.20
  34.1 1.3 %shard_map.184 = (f32[72,576]{1,0:T(8,128)S(1)}, bf16[72,576]{1,0:T(8,128)(2,1)S(1)}, bf16[72,576]{1,0:T(8,128)(2,1)S(1)}, bf16[72,576]{1,0:T(8,128)(2,1)}, bf16...) custom-call(s32[1]{0:T(128)} %bitcast.26.y_ref, ...), custom_call_target="tpu_custom_call" | custom-call | flops 800000000 | bytes 1048576 | tf_op jit(solution)/shard_map/pallas_call | solution.py:194
  35.4 0.7 copy-done.13
  36.0 3.2 %collective-permute-start.1 = (bf16[72,576]{1,0:T(8,128)(2,1)S(1)}, bf16[72,576]{1,0:T(8,128)(2,1)S(1)}, u32[]{:S(2)}, u32[]{:S(2)}) collective-permute-start(bf16[72,576]{1,0:T(8,128)(2,1)S(1)} %get-tuple-element.44), channel_id=1, source_target_pairs={{0,64},{64,128},{128,192},{192,256},{256,320},{320,384},{384,448},... | collective-permute-start | bytes 248840 | tf_op jit(solution)/shard_map/ppermute | solution.py:214
  39.2 4.2 %collective-permute-start.2 = (bf16[72,576]{1,0:T(8,128)(2,1)S(1)}, bf16[72,576]{1,0:T(8,128)(2,1)S(1)}, u32[]{:S(2)}, u32[]{:S(2)}) collective-permute-start(bf16[72,576]{1,0:T(8,128)(2,1)S(1)} %get-tuple-element.45), channel_id=1, source_target_pairs={{0,128},{64,192},{128,256},{192,320},{256,384},{320,448},{384,0},{... | collective-permute-start | bytes 248840 | tf_op jit(solution)/shard_map/ppermute | solution.py:214
  43.4 4.6 %collective-permute-start.3 = (bf16[72,576]{1,0:T(8,128)(2,1)}, bf16[72,576]{1,0:T(8,128)(2,1)S(1)}, u32[]{:S(2)}, u32[]{:S(2)}) collective-permute-start(bf16[72,576]{1,0:T(8,128)(2,1)} %get-tuple-element.46), channel_id=1, source_target_pairs={{0,192},{64,256},{128,320},{192,384},{256,448},{320,0},{384,64},{4... | collective-permute-start | bytes 248840 | tf_op jit(solution)/shard_map/ppermute | solution.py:214
  48.1 3.5 %collective-permute-start.4 = (bf16[72,576]{1,0:T(8,128)(2,1)S(1)}, bf16[72,576]{1,0:T(8,128)(2,1)S(1)}, u32[]{:S(2)}, u32[]{:S(2)}) collective-permute-start(bf16[72,576]{1,0:T(8,128)(2,1)S(1)} %get-tuple-element.47), channel_id=1, source_target_pairs={{0,256},{64,320},{128,384},{192,448},{256,0},{320,64},{384,128},{4... | collective-permute-start | bytes 248840 | tf_op jit(solution)/shard_map/ppermute | solution.py:214
  51.6 4.9 %collective-permute-start.5 = (bf16[72,576]{1,0:T(8,128)(2,1)S(1)}, bf16[72,576]{1,0:T(8,128)(2,1)}, u32[]{:S(2)}, u32[]{:S(2)}) collective-permute-start(bf16[72,576]{1,0:T(8,128)(2,1)S(1)} %get-tuple-element.48), channel_id=1, source_target_pairs={{0,320},{64,384},{128,448},{192,0},{256,64},{320,128},{384,192},{4... | collective-permute-start | bytes 248840 | tf_op jit(solution)/shard_map/ppermute | solution.py:214
  56.5 0.0 collective-permute-done.1.rest_0_
  56.5 5.0 %collective-permute-start.6 = (bf16[72,576]{1,0:T(8,128)(2,1)S(1)}, bf16[72,576]{1,0:T(8,128)(2,1)}, u32[]{:S(2)}, u32[]{:S(2)}) collective-permute-start(bf16[72,576]{1,0:T(8,128)(2,1)S(1)} %get-tuple-element.49), channel_id=1, source_target_pairs={{0,384},{64,448},{128,0},{192,64},{256,128},{320,192},{384,256},{4... | collective-permute-start | bytes 248840 | tf_op jit(solution)/shard_map/ppermute | solution.py:214
  61.5 0.0 collective-permute-done.2.rest_1_
  61.5 3.0 %collective-permute-start.7 = (bf16[72,576]{1,0:T(8,128)(2,1)S(1)}, bf16[72,576]{1,0:T(8,128)(2,1)}, u32[]{:S(2)}, u32[]{:S(2)}) collective-permute-start(bf16[72,576]{1,0:T(8,128)(2,1)S(1)} %get-tuple-element.50), channel_id=1, source_target_pairs={{0,448},{64,0},{128,64},{192,128},{256,192},{320,256},{384,320},{4... | collective-permute-start | bytes 248840 | tf_op jit(solution)/shard_map/ppermute | solution.py:214
  64.5 0.0 copy-done.8
  64.5 0.0 copy-done.9
  64.5 0.0 copy-done.10
  64.5 0.0 copy-start
  64.5 0.0 copy-start.1
  64.6 0.0 copy-start.4
  64.6 0.0 copy-start.11
  64.6 0.9 shard_map.181.att_ref
  65.5 0.0 copy-start.17
  65.5 0.7 copy-done.17
  66.1 0.0 copy-done
  66.2 0.0 copy-done.1
  66.2 0.0 copy-done.4
  66.2 0.0 copy-done.11
  66.2 0.0 copy-start.14
  66.2 0.9 shard_map.179
  67.0 0.0 copy-start.15
  67.0 0.0 copy-start.2
  67.1 0.0 copy-start.12
  67.1 0.0 copy-start.18
  67.1 0.0 collective-permute-done.3.rest_2_
  67.1 0.0 collective-permute-done.4.rest_3_
  67.1 0.0 collective-permute-done.5.rest_4_
  67.1 2.9 %collective-permute-done.6.rest_5_ = bf16[72,576]{1,0:T(8,128)(2,1)} collective-permute-done((bf16[72,576]{1,0:T(8,128)(2,1)S(1)}, bf16[72,576]{1,0:T(8,128)(2,1)}, u32[]{:S(2)}, u32[]{:S(2)}) %collective-permute-start.6) | collective-permute-done | bytes 82976 | tf_op jit(solution)/shard_map/ppermute | solution.py:214
  70.0 1.0 collective-permute-done.7.rest_6_
  71.0 0.0 copy-done.14
  71.0 1.1 shard_map.185
  72.1 0.0 copy-done.15
  72.1 2.2 %collective-permute-start.8 = (bf16[36,576]{1,0:T(8,128)(2,1)S(1)}, bf16[36,576]{1,0:T(8,128)(2,1)S(1)}, u32[]{:S(2)}, u32[]{:S(2)}) collective-permute-start(bf16[36,576]{1,0:T(8,128)(2,1)S(1)} %get-tuple-element.52), channel_id=1, source_target_pairs={{0,512},{512,0},{1,513},{513,1},{2,514},{514,2},{3,515},{515,3},{4... | collective-permute-start | bytes 124424 | tf_op jit(solution)/shard_map/ppermute | solution.py:210
  74.3 0.0 all-to-all-done.cot_ref
  74.4 0.9 shard_map.182
  75.2 0.0 copy-start.5
  75.3 0.0 copy-start.6
  75.3 0.0 copy-start.7
  75.3 0.0 copy-start.16
  75.3 3.4 %collective-permute-start.9 = (f32[1,1152]{1,0:T(1,128)S(1)}, f32[1,1152]{1,0:T(1,128)S(1)}, u32[]{:S(2)}, u32[]{:S(2)}) collective-permute-start(f32[1,1152]{1,0:T(1,128)S(1)} %broadcast_select_fusion.2), channel_id=1, source_target_pairs={{0,1},{1,0},{2,3},{3,2},{4,5},{5,4},{6,7},{7,6},{8,9},{9,8},{10,11... | collective-permute-start | bytes 13832 | tf_op jit(solution)/shard_map/ppermute | solution.py:210
  78.7 0.0 collective-permute-done.8.in_ref
  78.7 0.8 collective-permute-done.9.came_ref
  79.5 0.8 shard_map.186
  80.3 14.8 %all-to-all-start.1 = ((bf16[32,16,128]{2,1,0:T(8,128)(2,1)}), bf16[32,16,128]{2,1,0:T(8,128)(2,1)S(1)}, u32[]{:S(2)}, u32[]{:S(2)}) async-start(bf16[32,16,128]{2,1,0:T(8,128)(2,1)} %shard_map.186), calls=%async_computation.1 | async-start | bytes 262144 | tf_op jit(solution)/shard_map/all_to_all | solution.py:206
  95.2 3.2 %shard_map.180 = (bf16[64,2,576]{2,1,0:T(2,128)(2,1)}, bf16[64,2,576]{2,1,0:T(2,128)(2,1)}, bf16[64,2,576]{2,1,0:T(2,128)(2,1)}) custom-call(bf16[64,2,576]{2,1,0:T(2,128)(2,1)S(1)} %bitcast.37, bf16[64,2,576]{2,1,0:T(2,128)(2,1)S(1)} %bitcast.39, bf16[64,2,576]{2,1,0:T(2,128)(2,1)S(1)} %bitcast.41, bf16[1152,128]{1,0:T(8,128)(2,1)S(1)} %copy-done.4, ...), custom_call_target="tpu_custom_call" | custom-call | flops 1600000000 | bytes 1048576 | tf_op jit(solution)/shard_map/pallas_call | solution.py:194
  98.4 11.9 %all-to-all-done.1.in_ref = bf16[32,16,128]{2,1,0:T(8,128)(2,1)S(1)} async-done(((bf16[32,16,128]{2,1,0:T(8,128)(2,1)}), bf16[32,16,128]{2,1,0:T(8,128)(2,1)S(1)}, u32[]{:S(2)}, u32[]{:S(2)}) %all-to-all-start.1) | async-done | bytes 131104 | tf_op jit(solution)/shard_map/all_to_all | solution.py:206
  110.3 0.8 shard_map.187
  111.1 5.0 %collective-permute-start.10 = (f32[1,1152]{1,0:T(1,128)S(1)}, f32[1,1152]{1,0:T(1,128)S(1)}, u32[]{:S(2)}, u32[]{:S(2)}) collective-permute-start(f32[1,1152]{1,0:T(1,128)S(1)} %get-tuple-element.56), channel_id=1, source_target_pairs={{0,1},{1,0},{2,3},{3,2},{4,5},{5,4},{6,7},{7,6},{8,9},{9,8},{10,11... | collective-permute-start | bytes 13832 | tf_op jit(solution)/shard_map/ppermute | solution.py:210
  116.1 2.9 %shard_map.183 = (bf16[576,128]{1,0:T(8,128)(2,1)}, bf16[576,128]{1,0:T(8,128)(2,1)}, bf16[576,128]{1,0:T(8,128)(2,1)}) custom-call(bf16[576,128]{1,0:T(8,128)(2,1)S(1)} %bitcast.43, bf16[576,128]{1,0:T(8,128)(2,1)S(1)} %bitcast.45, bf16[576,128]{1,0:T(8,128)(2,1)S(1)} %bitcast.47, bf16[576,128]{1,0:T(8,128)(2,1)S(1)} %copy-done.19, ...), custom_call_target="tpu_custom_call" | custom-call | flops 1600000000 | bytes 1048576 | tf_op jit(solution)/shard_map/pallas_call | solution.py:194
  119.0 0.0 collective-permute-done.10
  119.0 0.6 broadcast_select_fusion
  (16 shorter events, 0.0 us)
Async XLA Ops:
  0.6 73.7 %all-to-all-start = ((bf16[64,2,1152]{2,1,0:T(2,128)(2,1)}), bf16[64,2,1152]{2,1,0:T(2,128)(2,1)S(1)}, u32[]{:S(2)}, u32[]{:S(2)}) async-start(bf16[64,2,1152]{2,1,0:T(2,128)(2,1)} %bitcast.31), calls=%async_computation | async-start | bytes 589824 | tf_op jit(solution)/shard_map/all_to_all | solution.py:206
  28.4 3.8 %collective-permute-start = (bf16[1152,128]{1,0:T(8,128)(2,1)}, bf16[1152,128]{1,0:T(8,128)(2,1)S(1)}, u32[]{:S(2)}, u32[]{:S(2)}) collective-permute-start(bf16[1152,128]{1,0:T(8,128)(2,1)} %get-tuple-element.33.att_ref.mine_ref), channel_id=1, source_target_pairs={{0,1},{1,0},{2,3},{3,2},{4,5},{5,4},{6,7},{7,6},{8,9},{9,8},{10,11... | collective-permute-start | bytes 884744 | tf_op jit(solution)/shard_map/ppermute | solution.py:210
  32.2 1.0 copy-start.3
  33.2 0.9 copy-start.20
  34.1 30.4 %copy-start.8 = (bf16[1,1,128,576]{2,3,1,0:T(8,128)(2,1)S(1)}, bf16[1,1,128,576]{2,3,1,0:T(8,128)(2,1)}, u32[]{:S(2)}) copy-start(bf16[1,1,128,576]{2,3,1,0:T(8,128)(2,1)} %param.15) | copy-start | bytes 442372
  34.1 30.4 %copy-start.9 = (bf16[1,1,128,576]{2,3,1,0:T(8,128)(2,1)S(1)}, bf16[1,1,128,576]{2,3,1,0:T(8,128)(2,1)}, u32[]{:S(2)}) copy-start(bf16[1,1,128,576]{2,3,1,0:T(8,128)(2,1)} %param.16) | copy-start | bytes 442372
  34.1 30.4 %copy-start.10 = (bf16[1,1,128,576]{2,3,1,0:T(8,128)(2,1)S(1)}, bf16[1,1,128,576]{2,3,1,0:T(8,128)(2,1)}, u32[]{:S(2)}) copy-start(bf16[1,1,128,576]{2,3,1,0:T(8,128)(2,1)} %param.17) | copy-start | bytes 442372
  35.3 0.7 copy-start.13
  36.0 20.5 %collective-permute-start.1 = (bf16[72,576]{1,0:T(8,128)(2,1)S(1)}, bf16[72,576]{1,0:T(8,128)(2,1)S(1)}, u32[]{:S(2)}, u32[]{:S(2)}) collective-permute-start(bf16[72,576]{1,0:T(8,128)(2,1)S(1)} %get-tuple-element.44), channel_id=1, source_target_pairs={{0,64},{64,128},{128,192},{192,256},{256,320},{320,384},{384,448},... | collective-permute-start | bytes 248840 | tf_op jit(solution)/shard_map/ppermute | solution.py:214
  39.2 22.3 %collective-permute-start.2 = (bf16[72,576]{1,0:T(8,128)(2,1)S(1)}, bf16[72,576]{1,0:T(8,128)(2,1)S(1)}, u32[]{:S(2)}, u32[]{:S(2)}) collective-permute-start(bf16[72,576]{1,0:T(8,128)(2,1)S(1)} %get-tuple-element.45), channel_id=1, source_target_pairs={{0,128},{64,192},{128,256},{192,320},{256,384},{320,448},{384,0},{... | collective-permute-start | bytes 248840 | tf_op jit(solution)/shard_map/ppermute | solution.py:214
  43.4 23.7 %collective-permute-start.3 = (bf16[72,576]{1,0:T(8,128)(2,1)}, bf16[72,576]{1,0:T(8,128)(2,1)S(1)}, u32[]{:S(2)}, u32[]{:S(2)}) collective-permute-start(bf16[72,576]{1,0:T(8,128)(2,1)} %get-tuple-element.46), channel_id=1, source_target_pairs={{0,192},{64,256},{128,320},{192,384},{256,448},{320,0},{384,64},{4... | collective-permute-start | bytes 248840 | tf_op jit(solution)/shard_map/ppermute | solution.py:214
  48.1 19.0 %collective-permute-start.4 = (bf16[72,576]{1,0:T(8,128)(2,1)S(1)}, bf16[72,576]{1,0:T(8,128)(2,1)S(1)}, u32[]{:S(2)}, u32[]{:S(2)}) collective-permute-start(bf16[72,576]{1,0:T(8,128)(2,1)S(1)} %get-tuple-element.47), channel_id=1, source_target_pairs={{0,256},{64,320},{128,384},{192,448},{256,0},{320,64},{384,128},{4... | collective-permute-start | bytes 248840 | tf_op jit(solution)/shard_map/ppermute | solution.py:214
  51.6 15.5 %collective-permute-start.5 = (bf16[72,576]{1,0:T(8,128)(2,1)S(1)}, bf16[72,576]{1,0:T(8,128)(2,1)}, u32[]{:S(2)}, u32[]{:S(2)}) collective-permute-start(bf16[72,576]{1,0:T(8,128)(2,1)S(1)} %get-tuple-element.48), channel_id=1, source_target_pairs={{0,320},{64,384},{128,448},{192,0},{256,64},{320,128},{384,192},{4... | collective-permute-start | bytes 248840 | tf_op jit(solution)/shard_map/ppermute | solution.py:214
  56.5 13.5 %collective-permute-start.6 = (bf16[72,576]{1,0:T(8,128)(2,1)S(1)}, bf16[72,576]{1,0:T(8,128)(2,1)}, u32[]{:S(2)}, u32[]{:S(2)}) collective-permute-start(bf16[72,576]{1,0:T(8,128)(2,1)S(1)} %get-tuple-element.49), channel_id=1, source_target_pairs={{0,384},{64,448},{128,0},{192,64},{256,128},{320,192},{384,256},{4... | collective-permute-start | bytes 248840 | tf_op jit(solution)/shard_map/ppermute | solution.py:214
  61.5 9.5 %collective-permute-start.7 = (bf16[72,576]{1,0:T(8,128)(2,1)S(1)}, bf16[72,576]{1,0:T(8,128)(2,1)}, u32[]{:S(2)}, u32[]{:S(2)}) collective-permute-start(bf16[72,576]{1,0:T(8,128)(2,1)S(1)} %get-tuple-element.50), channel_id=1, source_target_pairs={{0,448},{64,0},{128,64},{192,128},{256,192},{320,256},{384,320},{4... | collective-permute-start | bytes 248840 | tf_op jit(solution)/shard_map/ppermute | solution.py:214
  64.5 1.6 %copy-start = (bf16[1,64,2,1152]{3,2,1,0:T(2,128)(2,1)S(1)}, bf16[1,64,2,1152]{3,2,1,0:T(2,128)(2,1)}, u32[]{:S(2)}) copy-start(bf16[1,64,2,1152]{3,2,1,0:T(2,128)(2,1)} %param.11) | copy-start | bytes 884740
  64.5 1.6 %copy-start.1 = (bf16[1152,576]{0,1:T(8,128)(2,1)S(1)}, bf16[1152,576]{0,1:T(8,128)(2,1)}, u32[]{:S(2)}) copy-start(bf16[1152,576]{0,1:T(8,128)(2,1)} %param.18) | copy-start | bytes 3981316
  64.6 1.6 %copy-start.4 = (bf16[1152,128]{1,0:T(8,128)(2,1)S(1)}, bf16[1152,128]{1,0:T(8,128)(2,1)}, u32[]{:S(2)}) copy-start(bf16[1152,128]{1,0:T(8,128)(2,1)} %get-tuple-element.33.att_ref.mine_ref) | copy-start | bytes 884740
  64.6 1.6 %copy-start.11 = (f32[1,1152]{1,0:T(1,128)S(1)}, f32[1,1152]{1,0:T(1,128)}, u32[]{:S(2)}) copy-start(f32[1,1152]{1,0:T(1,128)} %gate_ref.4) | copy-start | bytes 13828
  65.5 0.7 copy-start.17
  66.2 4.8 %copy-start.14 = (f32[72,576]{1,0:T(8,128)S(1)}, f32[72,576]{1,0:T(8,128)}, u32[]{:S(2)}) copy-start(f32[72,576]{1,0:T(8,128)} %copy-done.13) | copy-start | bytes 497668
  67.0 5.1 %copy-start.15 = (bf16[576,128]{1,0:T(8,128)(2,1)}, bf16[576,128]{1,0:T(8,128)(2,1)S(1)}, u32[]{:S(2)}) copy-start(bf16[576,128]{1,0:T(8,128)(2,1)S(1)} %get-tuple-element.34.d_ref) | copy-start | bytes 442372
  67.0 7.3 %copy-start.2 = (bf16[1152,576]{0,1:T(8,128)(2,1)S(1)}, bf16[1152,576]{0,1:T(8,128)(2,1)}, u32[]{:S(2)}) copy-start(bf16[1152,576]{0,1:T(8,128)(2,1)} %param.19) | copy-start | bytes 3981316
  67.1 7.3 %copy-start.12 = (f32[1,1152]{1,0:T(1,128)S(1)}, f32[1,1152]{1,0:T(1,128)}, u32[]{:S(2)}) copy-start(f32[1,1152]{1,0:T(1,128)} %gate_ref.5) | copy-start | bytes 13828
  67.1 7.3 %copy-start.18 = (bf16[576,128]{1,0:T(8,128)(2,1)S(1)}, bf16[576,128]{1,0:T(8,128)(2,1)}, u32[]{:S(2)}) copy-start(bf16[576,128]{1,0:T(8,128)(2,1)} %copy-done.17) | copy-start | bytes 442372
  72.1 6.6 %collective-permute-start.8 = (bf16[36,576]{1,0:T(8,128)(2,1)S(1)}, bf16[36,576]{1,0:T(8,128)(2,1)S(1)}, u32[]{:S(2)}, u32[]{:S(2)}) collective-permute-start(bf16[36,576]{1,0:T(8,128)(2,1)S(1)} %get-tuple-element.52), channel_id=1, source_target_pairs={{0,512},{512,0},{1,513},{513,1},{2,514},{514,2},{3,515},{515,3},{4... | collective-permute-start | bytes 124424 | tf_op jit(solution)/shard_map/ppermute | solution.py:210
  75.2 19.9 %copy-start.5 = (bf16[1,64,2,576]{3,2,1,0:T(2,128)(2,1)S(1)}, bf16[1,64,2,576]{3,2,1,0:T(2,128)(2,1)}, u32[]{:S(2)}) copy-start(bf16[1,64,2,576]{3,2,1,0:T(2,128)(2,1)} %param.12) | copy-start | bytes 442372
  75.3 19.9 %copy-start.6 = (bf16[1,64,2,576]{3,2,1,0:T(2,128)(2,1)S(1)}, bf16[1,64,2,576]{3,2,1,0:T(2,128)(2,1)}, u32[]{:S(2)}) copy-start(bf16[1,64,2,576]{3,2,1,0:T(2,128)(2,1)} %param.13) | copy-start | bytes 442372
  75.3 19.9 %copy-start.7 = (bf16[1,64,2,576]{3,2,1,0:T(2,128)(2,1)S(1)}, bf16[1,64,2,576]{3,2,1,0:T(2,128)(2,1)}, u32[]{:S(2)}) copy-start(bf16[1,64,2,576]{3,2,1,0:T(2,128)(2,1)} %param.14) | copy-start | bytes 442372
  75.3 19.9 %copy-start.16 = (bf16[576,128]{1,0:T(8,128)(2,1)S(1)}, bf16[576,128]{1,0:T(8,128)(2,1)}, u32[]{:S(2)}) copy-start(bf16[576,128]{1,0:T(8,128)(2,1)} %copy-done.15) | copy-start | bytes 442372
  75.3 4.2 %collective-permute-start.9 = (f32[1,1152]{1,0:T(1,128)S(1)}, f32[1,1152]{1,0:T(1,128)S(1)}, u32[]{:S(2)}, u32[]{:S(2)}) collective-permute-start(f32[1,1152]{1,0:T(1,128)S(1)} %broadcast_select_fusion.2), channel_id=1, source_target_pairs={{0,1},{1,0},{2,3},{3,2},{4,5},{5,4},{6,7},{7,6},{8,9},{9,8},{10,11... | collective-permute-start | bytes 13832 | tf_op jit(solution)/shard_map/ppermute | solution.py:210
  80.3 30.0 %all-to-all-start.1 = ((bf16[32,16,128]{2,1,0:T(8,128)(2,1)}), bf16[32,16,128]{2,1,0:T(8,128)(2,1)S(1)}, u32[]{:S(2)}, u32[]{:S(2)}) async-start(bf16[32,16,128]{2,1,0:T(8,128)(2,1)} %shard_map.186), calls=%async_computation.1 | async-start | bytes 262144 | tf_op jit(solution)/shard_map/all_to_all | solution.py:206
  98.4 17.8 %copy-start.19 = (bf16[576,128]{1,0:T(8,128)(2,1)S(1)}, bf16[576,128]{1,0:T(8,128)(2,1)}, u32[]{:S(2)}) copy-start(bf16[576,128]{1,0:T(8,128)(2,1)} %copy-done.17) | copy-start | bytes 442372
  111.1 7.9 %collective-permute-start.10 = (f32[1,1152]{1,0:T(1,128)S(1)}, f32[1,1152]{1,0:T(1,128)S(1)}, u32[]{:S(2)}, u32[]{:S(2)}) collective-permute-start(f32[1,1152]{1,0:T(1,128)S(1)} %get-tuple-element.56), channel_id=1, source_target_pairs={{0,1},{1,0},{2,3},{3,2},{4,5},{5,4},{6,7},{7,6},{8,9},{9,8},{10,11... | collective-permute-start | bytes 13832 | tf_op jit(solution)/shard_map/ppermute | solution.py:210

commit v2 on v0

--- a/solution.py
+++ b/solution.py
@@ -53,6 +53,11 @@
     return ref[h * HD : (h + 1) * HD, :]
 
 
+def flat(ref):
+    x = ref[...]
+    return x.reshape(TOK, x.shape[-1])
+
+
 def forward_kernel(over_time, q_ref, k_ref, v_ref, out_ref, *turned_refs):
     keep = same_position() if over_time else None
     if over_time:
@@ -65,7 +70,7 @@
 
 
 def project_kernel(cot_ref, gate_ref, w_ref, att_ref, d_ref, part_ref):
-    cot = cot_ref[...].astype(F32)
+    cot = flat(cot_ref).astype(F32)
     gated = (cot * gate_ref[...]).astype(BF16)
     d_ref[...] = dot(w_ref[...], gated, NT).astype(BF16)
     projected = dot(att_ref[...], w_ref[...], TN)
@@ -74,7 +79,12 @@
 
 def backward_kernel(over_time, q_ref, k_ref, v_ref, att_ref, d_ref, gq_ref, gk_ref, gv_ref, *scratch):
     keep = same_position() if over_time else None
-    outs = scratch if over_time else (gq_ref, gk_ref, gv_ref)
+    outs = (gq_ref, gk_ref, gv_ref)
+    if over_time:
+        for src, dst in zip((q_ref, k_ref, v_ref), scratch):
+            dst[...] = turned(flat(src))
+        q_ref, k_ref, v_ref = scratch[:3]
+        outs = scratch[3:]
     for h in range(HEADS):
         sl = slice(h * HD, (h + 1) * HD)
         q, k, v, a, d = (rows_of(r, h) for r in (q_ref, k_ref, v_ref, att_ref, d_ref))
@@ -87,8 +97,8 @@
         for ref, g in zip(outs, grads):
             ref[sl, :] = g.astype(ref.dtype)
     if over_time:
-        for src, dst in zip(scratch, (gq_ref, gk_ref, gv_ref)):
-            dst[...] = src[...].T.astype(BF16)
+        for src, dst in zip(outs, (gq_ref, gk_ref, gv_ref)):
+            dst[...] = src[...].T.astype(BF16).reshape(dst.shape)
 
 
 def select_kernel(core_ref, own_ref, other_ref, gate_ref, out_ref):
@@ -99,7 +109,7 @@
     col = lax.broadcasted_iota(jnp.int32, (WIDTH, MODEL), 1)
     pick = jnp.where(col == channel, 1.0, 0.0).astype(BF16)
     for i, ref in enumerate((own_ref, other_ref)):
-        gated = (ref[...].astype(F32) * gate_ref[...]).astype(BF16)
+        gated = (flat(ref).astype(F32) * gate_ref[...]).astype(BF16)
         out_ref[:, i * TOK : (i + 1) * TOK] = dot(pick, gated, NT).astype(BF16)
 
 
@@ -109,16 +119,23 @@
     for ref, index in ((keep_ref, half), (send_ref, 1 - half)):
         rows = pl.ds(pl.multiple_of(index * 288, 32), 288)
         att = jnp.concatenate([own_ref[rows, :], other_ref[rows, :]], axis=1)
-        ref[...] = (dot(att, sel, NT) * norm).astype(ref.dtype)
+        term = dot(att, sel, NT) * norm
+        for y in range(8):
+            block = term[36 * y : 36 * y + 36]
+            tiles = [block[:, 128 * t : 128 * t + 128] for t in range(4)]
+            last = jnp.concatenate([block[:18, 512:], block[18:, 512:]], axis=1)
+            ref[y] = jnp.concatenate(tiles + [last], axis=0).astype(ref.dtype)
 
 
 def join_kernel(keep_ref, came_ref, out_ref):
-    total = (keep_ref[...] + came_ref[...].astype(F32)).astype(BF16)
-    out_ref[...] = total.reshape(out_ref.shape)
+    out_ref[...] = (keep_ref[...] + came_ref[...].astype(F32)).astype(BF16)
 
 
 def pack_kernel(core_ref, in_ref, time_ref, space_ref, came_ref, out_ref):
     total = jnp.sum(in_ref[...].astype(F32), axis=0)
+    last = jnp.concatenate([total[144:, :64], total[144:, 64:]], axis=0)
+    tiles = [total[36 * t : 36 * t + 36] for t in range(4)]
+    total = jnp.concatenate(tiles + [last], axis=1)
     total = jnp.concatenate([total, jnp.zeros((4, WIDTH), F32)], axis=0)
     gate = jnp.where(core_ref[0] == 0, time_ref[...], space_ref[...]) + came_ref[...]
     last = gate[:, 1024:]
@@ -183,33 +200,34 @@
     half = lax.axis_index("xl").astype(jnp.int32).reshape(1)
     exchanged = traded(cot[0], SEQ)
     other_cot = partner(cot, "c")
-    cot_t = cot.reshape(TOK, MODEL)
+    cot_t = cot[0]
     wt_t = wt.T
     ws_t = ws.T
+    turned_in = [pltpu.VMEM((WIDTH, TOK), BF16)] * 3
     q2, k2, v2 = (x.reshape(TOK, WIDTH) for x in (qt, kt, vt))
-    att_t, q_t, k_t, v_t = call(functools.partial(forward_kernel, True), [col] * 4, q2, k2, v2, flops=4 * US)
+    (att_t,) = call(functools.partial(forward_kernel, True), [col], q2, k2, v2, scratch=turned_in, flops=4 * US)
     other_att = partner(att_t, "c")
-    (selected,) = call(select_kernel, [((WIDTH, 2 * TOK), BF16)], core, cot_t, other_cot.reshape(TOK, MODEL), gt, scalars=1, flops=2 * US)
-    block = (288, WIDTH)
+    (selected,) = call(select_kernel, [((WIDTH, 2 * TOK), BF16)], core, cot_t, other_cot[0], gt, scalars=1, flops=2 * US)
+    block = (8, 162, 128)
     keep, send = call(functools.partial(product_kernel, norm_weight), [(block, F32), (block, BF16)], half, att_t, other_att, selected, scalars=1, flops=2 * US)
     came = partner(send, "xl")
-    (terms,) = call(join_kernel, [((8, 36, WIDTH), BF16)], keep, came, flops=US)
+    (terms,) = call(join_kernel, [(block, BF16)], keep, came, flops=US)
     arrived = traded(terms, "y")
     part = ((1, MODEL), F32)
     d_t, part_t = call(project_kernel, [col, part], cot_t, gt, wt_t, att_t, flops=2 * US)
     q_s, k_s, v_s = (swapped(x) for x in (qs, ks, vs))
     (att_s,) = call(functools.partial(forward_kernel, False), [col], q_s, k_s, v_s, flops=3 * US)
-    d_s, part_s = call(project_kernel, [col, part], exchanged.reshape(TOK, MODEL), gs, ws_t, att_s, flops=2 * US)
+    d_s, part_s = call(project_kernel, [col, part], exchanged, gs, ws_t, att_s, flops=2 * US)
     came_gate = partner(jnp.where(core == 0, part_s, part_t), "c")
     (packed,) = call(pack_kernel, [((32, 16, 128), BF16)], core, arrived, part_t, part_s, came_gate, scalars=1, flops=US)
     rows = traded(packed, ROWS)
-    tok = ((TOK, WIDTH), BF16)
-    grads_t = call(functools.partial(backward_kernel, True), [tok] * 3, q_t, k_t, v_t, att_t, d_t, scratch=[pltpu.VMEM((WIDTH, TOK), F32)] * 3, flops=4 * US)
+    tok = ((64, 2, WIDTH), BF16)
+    grads_t = call(functools.partial(backward_kernel, True), [tok] * 3, qt[0], kt[0], vt[0], att_t, d_t, scratch=turned_in + [pltpu.VMEM((WIDTH, TOK), F32)] * 3, flops=4 * US)
     grads_s = call(functools.partial(backward_kernel, False), [col] * 3, q_s, k_s, v_s, att_s, d_s, flops=4 * US)
     weight_grad, gate = call(functools.partial(finish_kernel, norm_gate), [((18, 36), F32), part], rows, flops=US)
     other_gate = partner(gate, "c")
     return (
-        *(g.reshape(1, 64, 2, WIDTH) for g in grads_t),
+        *(g[None] for g in grads_t),
         *(jnp.swapaxes(g, 0, 1)[None, None] for g in grads_s),
         weight_grad,
         jnp.where(core == 0, gate, other_gate),

time: 109 us -> 105 us (0.963)
  local copies, waits for them, and re-layouts: 10.9 us -> 2.7 us
  waiting for transfers between devices: 26.9 us -> 33.4 us
  starting transfers between devices: 56.3 us -> 53.6 us
  Pallas kernels: 12.5 us -> 13.7 us
    all_to_all x3, waiting for transfers between devices: 17.8 us -> 23.2 us  [traded(): return lax.all_to_all(x, axes, 0, 0, tiled=True)]
    unnamed x52 -> x22, local copies, waits for them, and re-layouts: 5.21 us -> 0.48 us
    reshape x6 -> x0, local copies, waits for them, and re-layouts: 3.51 us -> none  [the longest x3 2.21 us: step(): g.reshape(1, 64, 2, WIDTH)]
    all_to_all x3, starting transfers between devices: 41.2 us -> 38.7 us  [traded(): return lax.all_to_all(x, axes, 0, 0, tiled=True)]
    pallas_call x11, Pallas kernels: 12.5 us -> 13.7 us  [call(): pl.pallas_call(kernel, out_shape=shapes, in_specs=specs, out_specs=tuple(...]
  transfers between devices with their start and end apart: 8 -> 8, of which waited for: 6 -> 6; matrix products, arithmetic and copies ran while one was open for 5% -> 2% of each run, Pallas kernels for 10% -> 11%
where the time goes in v2:
time: 105 us
  starting transfers between devices  53.6 us (51%)
  waiting for transfers between devices  33.4 us (32%)
  Pallas kernels  13.7 us (13%)
  local copies, waits for them, and re-layouts  2.7 us (3%)
    all_to_all x3, starting transfers between devices, traded(): return lax.all_to_all(x, axes, 0, 0, tiled=True)  38.7 us
    all_to_all x3, waiting for transfers between devices, traded(): return lax.all_to_all(x, axes, 0, 0, tiled=True)  23.2 us
    ppermute x5, starting transfers between devices, partner(): return lax.ppermute(x, axis, [(0, 1), (1, 0)])  14.8 us
    pallas_call x11, Pallas kernels, call(): pl.pallas_call(kernel, out_shape=shapes, in_specs=specs, out_specs=tuple(...  13.7 us
    ppermute x5, waiting for transfers between devices, partner(): return lax.ppermute(x, axis, [(0, 1), (1, 0)])  10.2 us
    reshape x3, local copies, waits for them, and re-layouts, step(): q2, k2, v2 = (x.reshape(TOK, WIDTH) for x in (qt, kt, vt))  2.22 us
  transfers between devices with their start and end apart: 8, of which 6 were waited for; matrix products, arithmetic and copies ran while one was open for 2% of the time, Pallas kernels for 11%

profile of v2, /device:TPU:1, one launch (start us, length us, event | category | flops | bytes accessed | tf_op | source)
XLA Modules:
  0.0 104.9 jit_solution(11740235320278760464)
XLA Ops:
  0.6 0.0 copy-start.3
  0.7 23.4 %all-to-all-start = ((bf16[64,2,1152]{2,1,0:T(2,128)(2,1)}), bf16[64,2,1152]{2,1,0:T(2,128)(2,1)S(1)}, u32[]{:S(2)}, u32[]{:S(2)}) async-start(bf16[64,2,1152]{2,1,0:T(2,128)(2,1)} %bitcast.31), calls=%async_computation | async-start | bytes 589824 | tf_op jit(solution)/shard_map/all_to_all | solution.py:180
  24.1 2.4 %collective-permute-start.1 = (bf16[1,64,2,1152]{3,2,1,0:T(2,128)(2,1)}, bf16[1,64,2,1152]{3,2,1,0:T(2,128)(2,1)S(1)}, u32[]{:S(2)}, u32[]{:S(2)}) collective-permute-start(bf16[1,64,2,1152]{3,2,1,0:T(2,128)(2,1)} %param.11), channel_id=1, source_target_pairs={{0,1},{1,0},{2,3},{3,2},{4,5},{5,4},{6,7},{7,6},{8,9},{9,8},{10,11... | collective-permute-start | bytes 884744 | tf_op jit(solution)/shard_map/ppermute | solution.py:184
  26.4 1.0 reshape.36.q_ref
  27.5 1.0 reshape.37.k_ref
  28.5 0.0 copy-done.3
  28.5 0.1 reshape.38.v_ref
  28.7 0.0 copy-start
  28.7 0.0 copy-start.9
  28.7 1.0 %shard_map.178.att_ref.own_ref = bf16[576,128]{1,0:T(8,128)(2,1)S(1)} custom-call(bf16[128,576]{1,0:T(8,128)(2,1)S(1)} %reshape.36.q_ref, bf16[128,576]{1,0:T(8,128)(2,1)S(1)} %reshape.37.k_ref, bf16[128,576]{1,0:T(8,128)(2,1)S(1)} %reshape.38.v_ref), custom_call_target="tpu_custom_call" | custom-call | flops 1600000000 | bytes 1048576 | tf_op jit(solution)/shard_map/pallas_call | solution.py:168
  29.8 2.0 %collective-permute-start = (bf16[576,128]{1,0:T(8,128)(2,1)S(1)}, bf16[576,128]{1,0:T(8,128)(2,1)S(1)}, u32[]{:S(2)}, u32[]{:S(2)}) collective-permute-start(bf16[576,128]{1,0:T(8,128)(2,1)S(1)} %shard_map.178.att_ref.own_ref), channel_id=1, source_target_pairs={{0,1},{1,0},{2,3},{3,2},{4,5},{5,4},{6,7},{7,6},{8,9},{9,8},{10,11... | collective-permute-start | bytes 442376 | tf_op jit(solution)/shard_map/ppermute | solution.py:184
  31.7 0.0 collective-permute-done.1
  31.7 0.0 copy-done
  31.8 0.0 copy-done.9
  31.8 1.0 shard_map.184.sel_ref
  32.7 0.3 collective-permute-done.other_ref
  33.0 0.0 copy-start.6
  33.0 0.0 copy-start.7
  33.0 0.0 copy-start.8
  33.0 0.5 shard_map.185
  33.5 2.2 %collective-permute-start.2 = (bf16[8,162,128]{2,1,0:T(8,128)(2,1)S(1)}, bf16[8,162,128]{2,1,0:T(8,128)(2,1)S(1)}, u32[]{:S(2)}, u32[]{:S(2)}) collective-permute-start(bf16[8,162,128]{2,1,0:T(8,128)(2,1)S(1)} %get-tuple-element.32), channel_id=1, source_target_pairs={{0,512},{512,0},{1,513},{513,1},{2,514},{514,2},{3,515},{515,3},{4... | collective-permute-start | bytes 995336 | tf_op jit(solution)/shard_map/ppermute | solution.py:184
  35.8 0.0 copy-done.6
  35.8 0.0 copy-done.7
  35.8 0.0 copy-done.8
  35.8 0.9 shard_map.181.att_ref
  36.7 0.0 copy-start.4
  36.7 8.8 %collective-permute-done.2.came_ref = bf16[8,162,128]{2,1,0:T(8,128)(2,1)S(1)} collective-permute-done((bf16[8,162,128]{2,1,0:T(8,128)(2,1)S(1)}, bf16[8,162,128]{2,1,0:T(8,128)(2,1)S(1)}, u32[]{:S(2)}, u32[]{:S(2)}) %collective-permute-start.2) | collective-permute-done | bytes 331808 | tf_op jit(solution)/shard_map/ppermute | solution.py:184
  45.5 0.8 shard_map.186
  46.3 2.9 %all-to-all-done.cot_ref = bf16[64,2,1152]{2,1,0:T(2,128)(2,1)S(1)} async-done(((bf16[64,2,1152]{2,1,0:T(2,128)(2,1)}), bf16[64,2,1152]{2,1,0:T(2,128)(2,1)S(1)}, u32[]{:S(2)}, u32[]{:S(2)}) %all-to-all-start) | async-done | bytes 294944 | tf_op jit(solution)/shard_map/all_to_all | solution.py:180
  49.2 6.8 %all-to-all-start.1 = ((bf16[8,162,128]{2,1,0:T(8,128)(2,1)}), bf16[8,162,128]{2,1,0:T(8,128)(2,1)S(1)}, u32[]{:S(2)}, u32[]{:S(2)}) async-start(bf16[8,162,128]{2,1,0:T(8,128)(2,1)} %shard_map.186), calls=%async_computation.1 | async-start | bytes 688128 | tf_op jit(solution)/shard_map/all_to_all | solution.py:180
  56.0 0.0 copy-done.4
  56.0 0.0 copy-start.5
  56.0 0.0 copy-start.10
  56.0 0.9 shard_map.179
  56.9 0.4 copy-done.5
  57.3 0.0 copy-done.10
  57.3 0.8 shard_map.182
  58.2 0.0 copy-start.1
  58.2 0.0 copy-start.2
  58.2 2.1 %collective-permute-start.3 = (f32[1,1152]{1,0:T(1,128)S(1)}, f32[1,1152]{1,0:T(1,128)S(1)}, u32[]{:S(2)}, u32[]{:S(2)}) collective-permute-start(f32[1,1152]{1,0:T(1,128)S(1)} %broadcast_select_fusion.2), channel_id=1, source_target_pairs={{0,1},{1,0},{2,3},{3,2},{4,5},{5,4},{6,7},{7,6},{8,9},{9,8},{10,11... | collective-permute-start | bytes 13832 | tf_op jit(solution)/shard_map/ppermute | solution.py:184
  60.3 1.1 %collective-permute-done.3.came_ref = f32[1,1152]{1,0:T(1,128)S(1)} collective-permute-done((f32[1,1152]{1,0:T(1,128)S(1)}, f32[1,1152]{1,0:T(1,128)S(1)}, u32[]{:S(2)}, u32[]{:S(2)}) %collective-permute-start.3) | collective-permute-done | bytes 4640 | tf_op jit(solution)/shard_map/ppermute | solution.py:184
  61.4 8.8 %all-to-all-done.1.in_ref = bf16[8,162,128]{2,1,0:T(8,128)(2,1)S(1)} async-done(((bf16[8,162,128]{2,1,0:T(8,128)(2,1)}), bf16[8,162,128]{2,1,0:T(8,128)(2,1)S(1)}, u32[]{:S(2)}, u32[]{:S(2)}) %all-to-all-start.1) | async-done | bytes 331808 | tf_op jit(solution)/shard_map/all_to_all | solution.py:180
  70.2 0.9 shard_map.187
  71.0 8.5 %all-to-all-start.2 = ((bf16[32,16,128]{2,1,0:T(8,128)(2,1)}), bf16[32,16,128]{2,1,0:T(8,128)(2,1)S(1)}, u32[]{:S(2)}, u32[]{:S(2)}) async-start(bf16[32,16,128]{2,1,0:T(8,128)(2,1)} %shard_map.187), calls=%async_computation.2 | async-start | bytes 262144 | tf_op jit(solution)/shard_map/all_to_all | solution.py:180
  79.5 0.0 copy-done.1
  79.6 0.0 copy-done.2
  79.6 3.2 %shard_map.180 = (bf16[64,2,576]{2,1,0:T(2,128)(2,1)}, bf16[64,2,576]{2,1,0:T(2,128)(2,1)}, bf16[64,2,576]{2,1,0:T(2,128)(2,1)}) custom-call(bf16[64,2,576]{2,1,0:T(2,128)(2,1)S(1)} %bitcast.34, bf16[64,2,576]{2,1,0:T(2,128)(2,1)S(1)} %bitcast.35, bf16[64,2,576]{2,1,0:T(2,128)(2,1)S(1)} %bitcast.36, bf16[576,128]{1,0:T(8,128)(2,1)S(1)} %shard_map.178.att_ref.own_ref, ...), custom_call_target="tpu_custom_call" | custom-call | flops 1600000000 | bytes 1048576 | tf_op jit(solution)/shard_map/pallas_call | solution.py:168
  82.8 11.5 %all-to-all-done.2.in_ref = bf16[32,16,128]{2,1,0:T(8,128)(2,1)S(1)} async-done(((bf16[32,16,128]{2,1,0:T(8,128)(2,1)}), bf16[32,16,128]{2,1,0:T(8,128)(2,1)S(1)}, u32[]{:S(2)}, u32[]{:S(2)}) %all-to-all-start.2) | async-done | bytes 131104 | tf_op jit(solution)/shard_map/all_to_all | solution.py:180
  94.3 0.8 shard_map.188
  95.1 6.3 %collective-permute-start.4 = (f32[1,1152]{1,0:T(1,128)S(1)}, f32[1,1152]{1,0:T(1,128)S(1)}, u32[]{:S(2)}, u32[]{:S(2)}) collective-permute-start(f32[1,1152]{1,0:T(1,128)S(1)} %get-tuple-element.36), channel_id=1, source_target_pairs={{0,1},{1,0},{2,3},{3,2},{4,5},{5,4},{6,7},{7,6},{8,9},{9,8},{10,11... | collective-permute-start | bytes 13832 | tf_op jit(solution)/shard_map/ppermute | solution.py:184
  101.4 2.9 %shard_map.183 = (bf16[576,128]{1,0:T(8,128)(2,1)}, bf16[576,128]{1,0:T(8,128)(2,1)}, bf16[576,128]{1,0:T(8,128)(2,1)}) custom-call(bf16[576,128]{1,0:T(8,128)(2,1)S(1)} %bitcast.41, bf16[576,128]{1,0:T(8,128)(2,1)S(1)} %bitcast.43, bf16[576,128]{1,0:T(8,128)(2,1)S(1)} %bitcast.45, bf16[576,128]{1,0:T(8,128)(2,1)S(1)} %shard_map.181.att_ref, ...), custom_call_target="tpu_custom_call" | custom-call | flops 1600000000 | bytes 1048576 | tf_op jit(solution)/shard_map/pallas_call | solution.py:168
  104.3 0.0 collective-permute-done.4
  104.3 0.6 broadcast_select_fusion
  (1 shorter events, 0.0 us)
Async XLA Ops:
  0.6 27.9 %copy-start.3 = (bf16[1,64,2,576]{3,2,1,0:T(2,128)(2,1)S(1)}, bf16[1,64,2,576]{3,2,1,0:T(2,128)(2,1)}, u32[]{:S(2)}) copy-start(bf16[1,64,2,576]{3,2,1,0:T(2,128)(2,1)} %param.14) | copy-start | bytes 442372
  0.7 48.5 %all-to-all-start = ((bf16[64,2,1152]{2,1,0:T(2,128)(2,1)}), bf16[64,2,1152]{2,1,0:T(2,128)(2,1)S(1)}, u32[]{:S(2)}, u32[]{:S(2)}) async-start(bf16[64,2,1152]{2,1,0:T(2,128)(2,1)} %bitcast.31), calls=%async_computation | async-start | bytes 589824 | tf_op jit(solution)/shard_map/all_to_all | solution.py:180
  24.1 7.7 %collective-permute-start.1 = (bf16[1,64,2,1152]{3,2,1,0:T(2,128)(2,1)}, bf16[1,64,2,1152]{3,2,1,0:T(2,128)(2,1)S(1)}, u32[]{:S(2)}, u32[]{:S(2)}) collective-permute-start(bf16[1,64,2,1152]{3,2,1,0:T(2,128)(2,1)} %param.11), channel_id=1, source_target_pairs={{0,1},{1,0},{2,3},{3,2},{4,5},{5,4},{6,7},{7,6},{8,9},{9,8},{10,11... | collective-permute-start | bytes 884744 | tf_op jit(solution)/shard_map/ppermute | solution.py:184
  28.7 3.1 %copy-start = (bf16[1,64,2,1152]{3,2,1,0:T(2,128)(2,1)S(1)}, bf16[1,64,2,1152]{3,2,1,0:T(2,128)(2,1)}, u32[]{:S(2)}) copy-start(bf16[1,64,2,1152]{3,2,1,0:T(2,128)(2,1)} %param.11) | copy-start | bytes 884740
  28.7 3.1 %copy-start.9 = (f32[1,1152]{1,0:T(1,128)S(1)}, f32[1,1152]{1,0:T(1,128)}, u32[]{:S(2)}) copy-start(f32[1,1152]{1,0:T(1,128)} %gate_ref.5) | copy-start | bytes 13828
  29.8 3.3 %collective-permute-start = (bf16[576,128]{1,0:T(8,128)(2,1)S(1)}, bf16[576,128]{1,0:T(8,128)(2,1)S(1)}, u32[]{:S(2)}, u32[]{:S(2)}) collective-permute-start(bf16[576,128]{1,0:T(8,128)(2,1)S(1)} %shard_map.178.att_ref.own_ref), channel_id=1, source_target_pairs={{0,1},{1,0},{2,3},{3,2},{4,5},{5,4},{6,7},{7,6},{8,9},{9,8},{10,11... | collective-permute-start | bytes 442376 | tf_op jit(solution)/shard_map/ppermute | solution.py:184
  33.0 2.7 %copy-start.6 = (bf16[1,1,128,576]{2,3,1,0:T(8,128)(2,1)S(1)}, bf16[1,1,128,576]{2,3,1,0:T(8,128)(2,1)}, u32[]{:S(2)}) copy-start(bf16[1,1,128,576]{2,3,1,0:T(8,128)(2,1)} %param.15) | copy-start | bytes 442372
  33.0 2.7 %copy-start.7 = (bf16[1,1,128,576]{2,3,1,0:T(8,128)(2,1)S(1)}, bf16[1,1,128,576]{2,3,1,0:T(8,128)(2,1)}, u32[]{:S(2)}) copy-start(bf16[1,1,128,576]{2,3,1,0:T(8,128)(2,1)} %param.16) | copy-start | bytes 442372
  33.0 2.8 %copy-start.8 = (bf16[1,1,128,576]{2,3,1,0:T(8,128)(2,1)S(1)}, bf16[1,1,128,576]{2,3,1,0:T(8,128)(2,1)}, u32[]{:S(2)}) copy-start(bf16[1,1,128,576]{2,3,1,0:T(8,128)(2,1)} %param.17) | copy-start | bytes 442372
  33.5 11.9 %collective-permute-start.2 = (bf16[8,162,128]{2,1,0:T(8,128)(2,1)S(1)}, bf16[8,162,128]{2,1,0:T(8,128)(2,1)S(1)}, u32[]{:S(2)}, u32[]{:S(2)}) collective-permute-start(bf16[8,162,128]{2,1,0:T(8,128)(2,1)S(1)} %get-tuple-element.32), channel_id=1, source_target_pairs={{0,512},{512,0},{1,513},{513,1},{2,514},{514,2},{3,515},{515,3},{4... | collective-permute-start | bytes 995336 | tf_op jit(solution)/shard_map/ppermute | solution.py:184
  36.7 19.3 %copy-start.4 = (bf16[1152,576]{0,1:T(8,128)(2,1)S(1)}, bf16[1152,576]{0,1:T(8,128)(2,1)}, u32[]{:S(2)}) copy-start(bf16[1152,576]{0,1:T(8,128)(2,1)} %param.18) | copy-start | bytes 3981316
  49.2 21.0 %all-to-all-start.1 = ((bf16[8,162,128]{2,1,0:T(8,128)(2,1)}), bf16[8,162,128]{2,1,0:T(8,128)(2,1)S(1)}, u32[]{:S(2)}, u32[]{:S(2)}) async-start(bf16[8,162,128]{2,1,0:T(8,128)(2,1)} %shard_map.186), calls=%async_computation.1 | async-start | bytes 688128 | tf_op jit(solution)/shard_map/all_to_all | solution.py:180
  56.0 1.3 %copy-start.5 = (bf16[1152,576]{0,1:T(8,128)(2,1)S(1)}, bf16[1152,576]{0,1:T(8,128)(2,1)}, u32[]{:S(2)}) copy-start(bf16[1152,576]{0,1:T(8,128)(2,1)} %param.19) | copy-start | bytes 3981316
  56.0 1.3 %copy-start.10 = (f32[1,1152]{1,0:T(1,128)S(1)}, f32[1,1152]{1,0:T(1,128)}, u32[]{:S(2)}) copy-start(f32[1,1152]{1,0:T(1,128)} %gate_ref.4) | copy-start | bytes 13828
  58.2 21.4 %copy-start.1 = (bf16[1,64,2,576]{3,2,1,0:T(2,128)(2,1)S(1)}, bf16[1,64,2,576]{3,2,1,0:T(2,128)(2,1)}, u32[]{:S(2)}) copy-start(bf16[1,64,2,576]{3,2,1,0:T(2,128)(2,1)} %param.12) | copy-start | bytes 442372
  58.2 21.4 %copy-start.2 = (bf16[1,64,2,576]{3,2,1,0:T(2,128)(2,1)S(1)}, bf16[1,64,2,576]{3,2,1,0:T(2,128)(2,1)}, u32[]{:S(2)}) copy-start(bf16[1,64,2,576]{3,2,1,0:T(2,128)(2,1)} %param.13) | copy-start | bytes 442372
  58.2 3.2 %collective-permute-start.3 = (f32[1,1152]{1,0:T(1,128)S(1)}, f32[1,1152]{1,0:T(1,128)S(1)}, u32[]{:S(2)}, u32[]{:S(2)}) collective-permute-start(f32[1,1152]{1,0:T(1,128)S(1)} %broadcast_select_fusion.2), channel_id=1, source_target_pairs={{0,1},{1,0},{2,3},{3,2},{4,5},{5,4},{6,7},{7,6},{8,9},{9,8},{10,11... | collective-permute-start | bytes 13832 | tf_op jit(solution)/shard_map/ppermute | solution.py:184
  71.0 23.3 %all-to-all-start.2 = ((bf16[32,16,128]{2,1,0:T(8,128)(2,1)}), bf16[32,16,128]{2,1,0:T(8,128)(2,1)S(1)}, u32[]{:S(2)}, u32[]{:S(2)}) async-start(bf16[32,16,128]{2,1,0:T(8,128)(2,1)} %shard_map.187), calls=%async_computation.2 | async-start | bytes 262144 | tf_op jit(solution)/shard_map/all_to_all | solution.py:180
  95.1 9.2 %collective-permute-start.4 = (f32[1,1152]{1,0:T(1,128)S(1)}, f32[1,1152]{1,0:T(1,128)S(1)}, u32[]{:S(2)}, u32[]{:S(2)}) collective-permute-start(f32[1,1152]{1,0:T(1,128)S(1)} %get-tuple-element.36), channel_id=1, source_target_pairs={{0,1},{1,0},{2,3},{3,2},{4,5},{5,4},{6,7},{7,6},{8,9},{9,8},{10,11... | collective-permute-start | bytes 13832 | tf_op jit(solution)/shard_map/ppermute | solution.py:184

commit v3 on v2

--- a/solution.py
+++ b/solution.py
@@ -20,7 +20,8 @@
 NN = (((1,), (0,)), ((), ()))
 F32 = jnp.float32
 BF16 = jnp.bfloat16
-DP = ("xl", "y")
+DP = ("xl", "yh", "yl")
+PAIRS = ("xl", "yh")
 SEQ = ("z", "xh", "c")
 ROWS = ("z", "xh")
 SCALE = 1.0 / math.sqrt(HD)
@@ -113,18 +114,21 @@
         out_ref[:, i * TOK : (i + 1) * TOK] = dot(pick, gated, NT).astype(BF16)
 
 
+def packed_block(block):
+    tiles = [block[:, 128 * t : 128 * t + 128] for t in range(4)]
+    last = jnp.concatenate([block[:18, 512:], block[18:, 512:]], axis=1)
+    return jnp.concatenate(tiles + [last], axis=0)
+
+
 def product_kernel(norm, half_ref, own_ref, other_ref, sel_ref, keep_ref, send_ref):
-    half = half_ref[0]
-    sel = sel_ref[...]
-    for ref, index in ((keep_ref, half), (send_ref, 1 - half)):
-        rows = pl.ds(pl.multiple_of(index * 288, 32), 288)
-        att = jnp.concatenate([own_ref[rows, :], other_ref[rows, :]], axis=1)
-        term = dot(att, sel, NT) * norm
-        for y in range(8):
-            block = term[36 * y : 36 * y + 36]
-            tiles = [block[:, 128 * t : 128 * t + 128] for t in range(4)]
-            last = jnp.concatenate([block[:18, 512:], block[18:, 512:]], axis=1)
-            ref[y] = jnp.concatenate(tiles + [last], axis=0).astype(ref.dtype)
+    first = half_ref[0] == 0
+    att = jnp.concatenate([own_ref[...], other_ref[...]], axis=1)
+    term = dot(att, sel_ref[...], NT) * norm
+    for g in range(8):
+        low = packed_block(term[HD * g : HD * g + 36])
+        high = packed_block(term[HD * g + 36 : HD * g + HD])
+        keep_ref[g] = jnp.where(first, low, high)
+        send_ref[g] = jnp.where(first, high, low).astype(BF16)
 
 
 def join_kernel(keep_ref, came_ref, out_ref):
@@ -197,7 +201,7 @@
     norm_gate = 1.0 / math.sqrt(64 * 128)
     col = ((WIDTH, TOK), BF16)
     core = lax.axis_index("c").astype(jnp.int32).reshape(1)
-    half = lax.axis_index("xl").astype(jnp.int32).reshape(1)
+    half = lax.axis_index("yl").astype(jnp.int32).reshape(1)
     exchanged = traded(cot[0], SEQ)
     other_cot = partner(cot, "c")
     cot_t = cot[0]
@@ -210,9 +214,9 @@
     (selected,) = call(select_kernel, [((WIDTH, 2 * TOK), BF16)], core, cot_t, other_cot[0], gt, scalars=1, flops=2 * US)
     block = (8, 162, 128)
     keep, send = call(functools.partial(product_kernel, norm_weight), [(block, F32), (block, BF16)], half, att_t, other_att, selected, scalars=1, flops=2 * US)
-    came = partner(send, "xl")
+    came = partner(send, "yl")
     (terms,) = call(join_kernel, [(block, BF16)], keep, came, flops=US)
-    arrived = traded(terms, "y")
+    arrived = traded(terms, PAIRS)
     part = ((1, MODEL), F32)
     d_t, part_t = call(project_kernel, [col, part], cot_t, gt, wt_t, att_t, flops=2 * US)
     q_s, k_s, v_s = (swapped(x) for x in (qs, ks, vs))
@@ -236,7 +240,7 @@
 
 
 def solution(mesh):
-    fine = Mesh(np.array(mesh.devices).reshape(2, 8, 16, 2, 2), ("xl", "y", "z", "xh", "c"))
+    fine = Mesh(np.array(mesh.devices).reshape(2, 4, 2, 16, 2, 2), ("xl", "yh", "yl", "z", "xh", "c"))
     by_pos = P(DP, None, SEQ, None)
     by_frame = P(DP, SEQ, None, None)
     in_specs = (by_pos,) * 4 + (by_frame,) * 3 + (P(), P(), P(DP, None), P(DP, None))

time: 105 us -> 105 us (level)
  waiting for transfers between devices: 33.4 us -> 31.5 us
  starting transfers between devices: 53.6 us -> 55.1 us
    ppermute x5, waiting for transfers between devices: 10.2 us -> 8.53 us  [partner(): return lax.ppermute(x, axis, [(0, 1), (1, 0)])]
where the time goes in v3:
time: 105 us; the launch traced here: 104 us
  starting transfers between devices  55.1 us (52%)
  waiting for transfers between devices  31.5 us (30%)
  Pallas kernels  13.6 us (13%)
  local copies, waits for them, and re-layouts  2.71 us (3%)
    all_to_all x3, starting transfers between devices, traded(): return lax.all_to_all(x, axes, 0, 0, tiled=True)  39.5 us
    all_to_all x3, waiting for transfers between devices, traded(): return lax.all_to_all(x, axes, 0, 0, tiled=True)  23 us
    ppermute x5, starting transfers between devices, partner(): return lax.ppermute(x, axis, [(0, 1), (1, 0)])  15.5 us
    pallas_call x11, Pallas kernels, call(): pl.pallas_call(kernel, out_shape=shapes, in_specs=specs, out_specs=tuple(...  13.6 us
    ppermute x5, waiting for transfers between devices, partner(): return lax.ppermute(x, axis, [(0, 1), (1, 0)])  8.53 us
    reshape x3, local copies, waits for them, and re-layouts, step(): q2, k2, v2 = (x.reshape(TOK, WIDTH) for x in (qt, kt, vt))  2.22 us
  transfers between devices with their start and end apart: 8, of which 6 were waited for; matrix products, arithmetic and copies ran while one was open for 2% of the time, Pallas kernels for 11%

profile of v3, /device:TPU:1, one launch (start us, length us, event | category | flops | bytes accessed | tf_op | source)
XLA Modules:
  0.0 104.4 jit_solution(5432478333543780514)
XLA Ops:
  0.6 0.0 copy-start.3
  0.7 23.4 %all-to-all-start = ((bf16[64,2,1152]{2,1,0:T(2,128)(2,1)}), bf16[64,2,1152]{2,1,0:T(2,128)(2,1)S(1)}, u32[]{:S(2)}, u32[]{:S(2)}) async-start(bf16[64,2,1152]{2,1,0:T(2,128)(2,1)} %bitcast.31), calls=%async_computation | async-start | bytes 589824 | tf_op jit(solution)/shard_map/all_to_all | solution.py:184
  24.1 2.4 %collective-permute-start.1 = (bf16[1,64,2,1152]{3,2,1,0:T(2,128)(2,1)}, bf16[1,64,2,1152]{3,2,1,0:T(2,128)(2,1)S(1)}, u32[]{:S(2)}, u32[]{:S(2)}) collective-permute-start(bf16[1,64,2,1152]{3,2,1,0:T(2,128)(2,1)} %param.11), channel_id=1, source_target_pairs={{0,1},{1,0},{2,3},{3,2},{4,5},{5,4},{6,7},{7,6},{8,9},{9,8},{10,11... | collective-permute-start | bytes 884744 | tf_op jit(solution)/shard_map/ppermute | solution.py:188
  26.4 1.0 %reshape.36.q_ref = bf16[128,576]{1,0:T(8,128)(2,1)S(1)} reshape(bf16[1,64,2,576]{3,2,1,0:T(2,128)(2,1)} %param.12) | data formatting | bytes 294912 | tf_op jit(solution)/shard_map/reshape | solution.py:211
  27.5 1.0 %reshape.37.k_ref = bf16[128,576]{1,0:T(8,128)(2,1)S(1)} reshape(bf16[1,64,2,576]{3,2,1,0:T(2,128)(2,1)} %param.13) | data formatting | bytes 294912 | tf_op jit(solution)/shard_map/reshape | solution.py:211
  28.5 0.0 copy-done.3
  28.5 0.1 reshape.38.v_ref
  28.7 0.0 copy-start
  28.7 0.0 copy-start.9
  28.7 1.0 %shard_map.178.att_ref.own_ref = bf16[576,128]{1,0:T(8,128)(2,1)S(1)} custom-call(bf16[128,576]{1,0:T(8,128)(2,1)S(1)} %reshape.36.q_ref, bf16[128,576]{1,0:T(8,128)(2,1)S(1)} %reshape.37.k_ref, bf16[128,576]{1,0:T(8,128)(2,1)S(1)} %reshape.38.v_ref), custom_call_target="tpu_custom_call" | custom-call | flops 1600000000 | bytes 1048576 | tf_op jit(solution)/shard_map/pallas_call | solution.py:172
  29.8 2.0 %collective-permute-start = (bf16[576,128]{1,0:T(8,128)(2,1)S(1)}, bf16[576,128]{1,0:T(8,128)(2,1)S(1)}, u32[]{:S(2)}, u32[]{:S(2)}) collective-permute-start(bf16[576,128]{1,0:T(8,128)(2,1)S(1)} %shard_map.178.att_ref.own_ref), channel_id=1, source_target_pairs={{0,1},{1,0},{2,3},{3,2},{4,5},{5,4},{6,7},{7,6},{8,9},{9,8},{10,11... | collective-permute-start | bytes 442376 | tf_op jit(solution)/shard_map/ppermute | solution.py:188
  31.7 0.0 collective-permute-done.1
  31.7 0.0 copy-done
  31.8 0.0 copy-done.9
  31.8 1.0 shard_map.184.sel_ref
  32.7 0.3 collective-permute-done.other_ref
  33.0 0.0 copy-start.6
  33.0 0.0 copy-start.7
  33.0 0.0 copy-start.8
  33.0 0.5 shard_map.185
  33.5 3.2 %collective-permute-start.2 = (bf16[8,162,128]{2,1,0:T(8,128)(2,1)S(1)}, bf16[8,162,128]{2,1,0:T(8,128)(2,1)S(1)}, u32[]{:S(2)}, u32[]{:S(2)}) collective-permute-start(bf16[8,162,128]{2,1,0:T(8,128)(2,1)S(1)} %get-tuple-element.32), channel_id=1, source_target_pairs={{0,64},{64,0},{1,65},{65,1},{2,66},{66,2},{3,67},{67,3},{4,68},{68... | collective-permute-start | bytes 995336 | tf_op jit(solution)/shard_map/ppermute | solution.py:188
  36.8 0.0 copy-done.6
  36.8 0.0 copy-done.7
  36.8 0.0 copy-done.8
  36.8 0.9 shard_map.181.att_ref
  37.7 0.0 copy-start.4
  37.7 7.1 %collective-permute-done.2.came_ref = bf16[8,162,128]{2,1,0:T(8,128)(2,1)S(1)} collective-permute-done((bf16[8,162,128]{2,1,0:T(8,128)(2,1)S(1)}, bf16[8,162,128]{2,1,0:T(8,128)(2,1)S(1)}, u32[]{:S(2)}, u32[]{:S(2)}) %collective-permute-start.2) | collective-permute-done | bytes 331808 | tf_op jit(solution)/shard_map/ppermute | solution.py:188
  44.8 0.8 shard_map.186
  45.6 3.6 %all-to-all-done.cot_ref = bf16[64,2,1152]{2,1,0:T(2,128)(2,1)S(1)} async-done(((bf16[64,2,1152]{2,1,0:T(2,128)(2,1)}), bf16[64,2,1152]{2,1,0:T(2,128)(2,1)S(1)}, u32[]{:S(2)}, u32[]{:S(2)}) %all-to-all-start) | async-done | bytes 294944 | tf_op jit(solution)/shard_map/all_to_all | solution.py:184
  49.2 6.8 %all-to-all-start.1 = ((bf16[8,162,128]{2,1,0:T(8,128)(2,1)}), bf16[8,162,128]{2,1,0:T(8,128)(2,1)S(1)}, u32[]{:S(2)}, u32[]{:S(2)}) async-start(bf16[8,162,128]{2,1,0:T(8,128)(2,1)} %shard_map.186), calls=%async_computation.1 | async-start | bytes 688128 | tf_op jit(solution)/shard_map/all_to_all | solution.py:184
  56.0 0.0 copy-done.4
  56.0 0.0 copy-start.5
  56.1 0.0 copy-start.10
  56.1 0.9 shard_map.179
  56.9 0.4 copy-done.5
  57.4 0.0 copy-done.10
  57.4 0.8 shard_map.182
  58.2 0.0 copy-start.1
  58.2 0.0 copy-start.2
  58.2 2.1 %collective-permute-start.3 = (f32[1,1152]{1,0:T(1,128)S(1)}, f32[1,1152]{1,0:T(1,128)S(1)}, u32[]{:S(2)}, u32[]{:S(2)}) collective-permute-start(f32[1,1152]{1,0:T(1,128)S(1)} %broadcast_select_fusion.2), channel_id=1, source_target_pairs={{0,1},{1,0},{2,3},{3,2},{4,5},{5,4},{6,7},{7,6},{8,9},{9,8},{10,11... | collective-permute-start | bytes 13832 | tf_op jit(solution)/shard_map/ppermute | solution.py:188
  60.3 1.1 %collective-permute-done.3.came_ref = f32[1,1152]{1,0:T(1,128)S(1)} collective-permute-done((f32[1,1152]{1,0:T(1,128)S(1)}, f32[1,1152]{1,0:T(1,128)S(1)}, u32[]{:S(2)}, u32[]{:S(2)}) %collective-permute-start.3) | collective-permute-done | bytes 4640 | tf_op jit(solution)/shard_map/ppermute | solution.py:188
  61.4 7.8 %all-to-all-done.1.in_ref = bf16[8,162,128]{2,1,0:T(8,128)(2,1)S(1)} async-done(((bf16[8,162,128]{2,1,0:T(8,128)(2,1)}), bf16[8,162,128]{2,1,0:T(8,128)(2,1)S(1)}, u32[]{:S(2)}, u32[]{:S(2)}) %all-to-all-start.1) | async-done | bytes 331808 | tf_op jit(solution)/shard_map/all_to_all | solution.py:184
  69.3 0.9 shard_map.187
  70.1 9.3 %all-to-all-start.2 = ((bf16[32,16,128]{2,1,0:T(8,128)(2,1)}), bf16[32,16,128]{2,1,0:T(8,128)(2,1)S(1)}, u32[]{:S(2)}, u32[]{:S(2)}) async-start(bf16[32,16,128]{2,1,0:T(8,128)(2,1)} %shard_map.187), calls=%async_computation.2 | async-start | bytes 262144 | tf_op jit(solution)/shard_map/all_to_all | solution.py:184
  79.4 0.0 copy-done.1
  79.4 0.0 copy-done.2
  79.4 3.2 %shard_map.180 = (bf16[64,2,576]{2,1,0:T(2,128)(2,1)}, bf16[64,2,576]{2,1,0:T(2,128)(2,1)}, bf16[64,2,576]{2,1,0:T(2,128)(2,1)}) custom-call(bf16[64,2,576]{2,1,0:T(2,128)(2,1)S(1)} %bitcast.34, bf16[64,2,576]{2,1,0:T(2,128)(2,1)S(1)} %bitcast.35, bf16[64,2,576]{2,1,0:T(2,128)(2,1)S(1)} %bitcast.36, bf16[576,128]{1,0:T(8,128)(2,1)S(1)} %shard_map.178.att_ref.own_ref, ...), custom_call_target="tpu_custom_call" | custom-call | flops 1600000000 | bytes 1048576 | tf_op jit(solution)/shard_map/pallas_call | solution.py:172
  82.6 11.5 %all-to-all-done.2.in_ref = bf16[32,16,128]{2,1,0:T(8,128)(2,1)S(1)} async-done(((bf16[32,16,128]{2,1,0:T(8,128)(2,1)}), bf16[32,16,128]{2,1,0:T(8,128)(2,1)S(1)}, u32[]{:S(2)}, u32[]{:S(2)}) %all-to-all-start.2) | async-done | bytes 131104 | tf_op jit(solution)/shard_map/all_to_all | solution.py:184
  94.2 0.8 shard_map.188
  95.0 5.9 %collective-permute-start.4 = (f32[1,1152]{1,0:T(1,128)S(1)}, f32[1,1152]{1,0:T(1,128)S(1)}, u32[]{:S(2)}, u32[]{:S(2)}) collective-permute-start(f32[1,1152]{1,0:T(1,128)S(1)} %get-tuple-element.36), channel_id=1, source_target_pairs={{0,1},{1,0},{2,3},{3,2},{4,5},{5,4},{6,7},{7,6},{8,9},{9,8},{10,11... | collective-permute-start | bytes 13832 | tf_op jit(solution)/shard_map/ppermute | solution.py:188
  100.9 2.9 %shard_map.183 = (bf16[576,128]{1,0:T(8,128)(2,1)}, bf16[576,128]{1,0:T(8,128)(2,1)}, bf16[576,128]{1,0:T(8,128)(2,1)}) custom-call(bf16[576,128]{1,0:T(8,128)(2,1)S(1)} %bitcast.41, bf16[576,128]{1,0:T(8,128)(2,1)S(1)} %bitcast.43, bf16[576,128]{1,0:T(8,128)(2,1)S(1)} %bitcast.45, bf16[576,128]{1,0:T(8,128)(2,1)S(1)} %shard_map.181.att_ref, ...), custom_call_target="tpu_custom_call" | custom-call | flops 1600000000 | bytes 1048576 | tf_op jit(solution)/shard_map/pallas_call | solution.py:172
  103.8 0.0 collective-permute-done.4
  103.8 0.6 broadcast_select_fusion
  (1 shorter events, 0.0 us)
Async XLA Ops:
  0.6 27.9 %copy-start.3 = (bf16[1,64,2,576]{3,2,1,0:T(2,128)(2,1)S(1)}, bf16[1,64,2,576]{3,2,1,0:T(2,128)(2,1)}, u32[]{:S(2)}) copy-start(bf16[1,64,2,576]{3,2,1,0:T(2,128)(2,1)} %param.14) | copy-start | bytes 442372
  0.7 48.5 %all-to-all-start = ((bf16[64,2,1152]{2,1,0:T(2,128)(2,1)}), bf16[64,2,1152]{2,1,0:T(2,128)(2,1)S(1)}, u32[]{:S(2)}, u32[]{:S(2)}) async-start(bf16[64,2,1152]{2,1,0:T(2,128)(2,1)} %bitcast.31), calls=%async_computation | async-start | bytes 589824 | tf_op jit(solution)/shard_map/all_to_all | solution.py:184
  24.1 7.7 %collective-permute-start.1 = (bf16[1,64,2,1152]{3,2,1,0:T(2,128)(2,1)}, bf16[1,64,2,1152]{3,2,1,0:T(2,128)(2,1)S(1)}, u32[]{:S(2)}, u32[]{:S(2)}) collective-permute-start(bf16[1,64,2,1152]{3,2,1,0:T(2,128)(2,1)} %param.11), channel_id=1, source_target_pairs={{0,1},{1,0},{2,3},{3,2},{4,5},{5,4},{6,7},{7,6},{8,9},{9,8},{10,11... | collective-permute-start | bytes 884744 | tf_op jit(solution)/shard_map/ppermute | solution.py:188
  28.7 3.1 %copy-start = (bf16[1,64,2,1152]{3,2,1,0:T(2,128)(2,1)S(1)}, bf16[1,64,2,1152]{3,2,1,0:T(2,128)(2,1)}, u32[]{:S(2)}) copy-start(bf16[1,64,2,1152]{3,2,1,0:T(2,128)(2,1)} %param.11) | copy-start | bytes 884740
  28.7 3.1 %copy-start.9 = (f32[1,1152]{1,0:T(1,128)S(1)}, f32[1,1152]{1,0:T(1,128)}, u32[]{:S(2)}) copy-start(f32[1,1152]{1,0:T(1,128)} %gate_ref.5) | copy-start | bytes 13828
  29.8 3.3 %collective-permute-start = (bf16[576,128]{1,0:T(8,128)(2,1)S(1)}, bf16[576,128]{1,0:T(8,128)(2,1)S(1)}, u32[]{:S(2)}, u32[]{:S(2)}) collective-permute-start(bf16[576,128]{1,0:T(8,128)(2,1)S(1)} %shard_map.178.att_ref.own_ref), channel_id=1, source_target_pairs={{0,1},{1,0},{2,3},{3,2},{4,5},{5,4},{6,7},{7,6},{8,9},{9,8},{10,11... | collective-permute-start | bytes 442376 | tf_op jit(solution)/shard_map/ppermute | solution.py:188
  33.0 3.7 %copy-start.6 = (bf16[1,1,128,576]{2,3,1,0:T(8,128)(2,1)S(1)}, bf16[1,1,128,576]{2,3,1,0:T(8,128)(2,1)}, u32[]{:S(2)}) copy-start(bf16[1,1,128,576]{2,3,1,0:T(8,128)(2,1)} %param.15) | copy-start | bytes 442372
  33.0 3.7 %copy-start.7 = (bf16[1,1,128,576]{2,3,1,0:T(8,128)(2,1)S(1)}, bf16[1,1,128,576]{2,3,1,0:T(8,128)(2,1)}, u32[]{:S(2)}) copy-start(bf16[1,1,128,576]{2,3,1,0:T(8,128)(2,1)} %param.16) | copy-start | bytes 442372
  33.0 3.7 %copy-start.8 = (bf16[1,1,128,576]{2,3,1,0:T(8,128)(2,1)S(1)}, bf16[1,1,128,576]{2,3,1,0:T(8,128)(2,1)}, u32[]{:S(2)}) copy-start(bf16[1,1,128,576]{2,3,1,0:T(8,128)(2,1)} %param.17) | copy-start | bytes 442372
  33.5 11.3 %collective-permute-start.2 = (bf16[8,162,128]{2,1,0:T(8,128)(2,1)S(1)}, bf16[8,162,128]{2,1,0:T(8,128)(2,1)S(1)}, u32[]{:S(2)}, u32[]{:S(2)}) collective-permute-start(bf16[8,162,128]{2,1,0:T(8,128)(2,1)S(1)} %get-tuple-element.32), channel_id=1, source_target_pairs={{0,64},{64,0},{1,65},{65,1},{2,66},{66,2},{3,67},{67,3},{4,68},{68... | collective-permute-start | bytes 995336 | tf_op jit(solution)/shard_map/ppermute | solution.py:188
  37.7 18.4 %copy-start.4 = (bf16[1152,576]{0,1:T(8,128)(2,1)S(1)}, bf16[1152,576]{0,1:T(8,128)(2,1)}, u32[]{:S(2)}) copy-start(bf16[1152,576]{0,1:T(8,128)(2,1)} %param.18) | copy-start | bytes 3981316
  49.2 20.1 %all-to-all-start.1 = ((bf16[8,162,128]{2,1,0:T(8,128)(2,1)}), bf16[8,162,128]{2,1,0:T(8,128)(2,1)S(1)}, u32[]{:S(2)}, u32[]{:S(2)}) async-start(bf16[8,162,128]{2,1,0:T(8,128)(2,1)} %shard_map.186), calls=%async_computation.1 | async-start | bytes 688128 | tf_op jit(solution)/shard_map/all_to_all | solution.py:184
  56.0 1.3 %copy-start.5 = (bf16[1152,576]{0,1:T(8,128)(2,1)S(1)}, bf16[1152,576]{0,1:T(8,128)(2,1)}, u32[]{:S(2)}) copy-start(bf16[1152,576]{0,1:T(8,128)(2,1)} %param.19) | copy-start | bytes 3981316
  56.1 1.3 %copy-start.10 = (f32[1,1152]{1,0:T(1,128)S(1)}, f32[1,1152]{1,0:T(1,128)}, u32[]{:S(2)}) copy-start(f32[1,1152]{1,0:T(1,128)} %gate_ref.4) | copy-start | bytes 13828
  58.2 21.2 %copy-start.1 = (bf16[1,64,2,576]{3,2,1,0:T(2,128)(2,1)S(1)}, bf16[1,64,2,576]{3,2,1,0:T(2,128)(2,1)}, u32[]{:S(2)}) copy-start(bf16[1,64,2,576]{3,2,1,0:T(2,128)(2,1)} %param.12) | copy-start | bytes 442372
  58.2 21.2 %copy-start.2 = (bf16[1,64,2,576]{3,2,1,0:T(2,128)(2,1)S(1)}, bf16[1,64,2,576]{3,2,1,0:T(2,128)(2,1)}, u32[]{:S(2)}) copy-start(bf16[1,64,2,576]{3,2,1,0:T(2,128)(2,1)} %param.13) | copy-start | bytes 442372
  58.2 3.2 %collective-permute-start.3 = (f32[1,1152]{1,0:T(1,128)S(1)}, f32[1,1152]{1,0:T(1,128)S(1)}, u32[]{:S(2)}, u32[]{:S(2)}) collective-permute-start(f32[1,1152]{1,0:T(1,128)S(1)} %broadcast_select_fusion.2), channel_id=1, source_target_pairs={{0,1},{1,0},{2,3},{3,2},{4,5},{5,4},{6,7},{7,6},{8,9},{9,8},{10,11... | collective-permute-start | bytes 13832 | tf_op jit(solution)/shard_map/ppermute | solution.py:188
  70.1 24.0 %all-to-all-start.2 = ((bf16[32,16,128]{2,1,0:T(8,128)(2,1)}), bf16[32,16,128]{2,1,0:T(8,128)(2,1)S(1)}, u32[]{:S(2)}, u32[]{:S(2)}) async-start(bf16[32,16,128]{2,1,0:T(8,128)(2,1)} %shard_map.187), calls=%async_computation.2 | async-start | bytes 262144 | tf_op jit(solution)/shard_map/all_to_all | solution.py:184
  95.0 8.8 %collective-permute-start.4 = (f32[1,1152]{1,0:T(1,128)S(1)}, f32[1,1152]{1,0:T(1,128)S(1)}, u32[]{:S(2)}, u32[]{:S(2)}) collective-permute-start(f32[1,1152]{1,0:T(1,128)S(1)} %get-tuple-element.36), channel_id=1, source_target_pairs={{0,1},{1,0},{2,3},{3,2},{4,5},{5,4},{6,7},{7,6},{8,9},{9,8},{10,11... | collective-permute-start | bytes 13832 | tf_op jit(solution)/shard_map/ppermute | solution.py:188

commit v4 on v3

--- a/solution.py
+++ b/solution.py
@@ -21,7 +21,6 @@
 F32 = jnp.float32
 BF16 = jnp.bfloat16
 DP = ("xl", "yh", "yl")
-PAIRS = ("xl", "yh")
 SEQ = ("z", "xh", "c")
 ROWS = ("z", "xh")
 SCALE = 1.0 / math.sqrt(HD)
@@ -120,19 +119,28 @@
     return jnp.concatenate(tiles + [last], axis=0)
 
 
-def product_kernel(norm, half_ref, own_ref, other_ref, sel_ref, keep_ref, send_ref):
-    first = half_ref[0] == 0
+def product_kernel(norm, half_ref, side_ref, own_ref, other_ref, sel_ref, keep_ref, x_ref, y_ref, d_ref):
+    first_y = half_ref[0] == 0
+    first_x = side_ref[0] == 0
     att = jnp.concatenate([own_ref[...], other_ref[...]], axis=1)
     term = dot(att, sel_ref[...], NT) * norm
-    for g in range(8):
-        low = packed_block(term[HD * g : HD * g + 36])
-        high = packed_block(term[HD * g + 36 : HD * g + HD])
-        keep_ref[g] = jnp.where(first, low, high)
-        send_ref[g] = jnp.where(first, high, low).astype(BF16)
-
-
-def join_kernel(keep_ref, came_ref, out_ref):
-    out_ref[...] = (keep_ref[...] + came_ref[...].astype(F32)).astype(BF16)
+    for g in range(4):
+        at = [288 * x + HD * g + 36 * y for x in (0, 1) for y in (0, 1)]
+        b00, b01, b10, b11 = (packed_block(term[i : i + 36]) for i in at)
+        mine = (jnp.where(first_x, b00, b10), jnp.where(first_x, b01, b11))
+        theirs = (jnp.where(first_x, b10, b00), jnp.where(first_x, b11, b01))
+        keep_ref[g] = jnp.where(first_y, mine[0], mine[1])
+        y_ref[g] = jnp.where(first_y, mine[1], mine[0]).astype(BF16)
+        x_ref[g] = jnp.where(first_y, theirs[0], theirs[1]).astype(BF16)
+        d_ref[g] = jnp.where(first_y, theirs[1], theirs[0]).astype(BF16)
+
+
+def join_kernel(keep_ref, *rest):
+    came, out_ref = rest[:3], rest[3]
+    total = keep_ref[...]
+    for ref in came:
+        total = total + ref[...].astype(F32)
+    out_ref[...] = total.astype(BF16)
 
 
 def pack_kernel(core_ref, in_ref, time_ref, space_ref, came_ref, out_ref):
@@ -202,6 +210,7 @@
     col = ((WIDTH, TOK), BF16)
     core = lax.axis_index("c").astype(jnp.int32).reshape(1)
     half = lax.axis_index("yl").astype(jnp.int32).reshape(1)
+    side = lax.axis_index("xl").astype(jnp.int32).reshape(1)
     exchanged = traded(cot[0], SEQ)
     other_cot = partner(cot, "c")
     cot_t = cot[0]
@@ -212,11 +221,13 @@
     (att_t,) = call(functools.partial(forward_kernel, True), [col], q2, k2, v2, scratch=turned_in, flops=4 * US)
     other_att = partner(att_t, "c")
     (selected,) = call(select_kernel, [((WIDTH, 2 * TOK), BF16)], core, cot_t, other_cot[0], gt, scalars=1, flops=2 * US)
-    block = (8, 162, 128)
-    keep, send = call(functools.partial(product_kernel, norm_weight), [(block, F32), (block, BF16)], half, att_t, other_att, selected, scalars=1, flops=2 * US)
-    came = partner(send, "yl")
-    (terms,) = call(join_kernel, [(block, BF16)], keep, came, flops=US)
-    arrived = traded(terms, PAIRS)
+    block = (4, 162, 128)
+    keep, to_x, to_y, to_d = call(functools.partial(product_kernel, norm_weight), [(block, F32)] + [(block, BF16)] * 3, half, side, att_t, other_att, selected, scalars=2, flops=2 * US)
+    came_d = lax.ppermute(to_d, ("xl", "yl"), [(i, 3 - i) for i in range(4)])
+    came_x = partner(to_x, "xl")
+    came_y = partner(to_y, "yl")
+    (terms,) = call(join_kernel, [(block, BF16)], keep, came_x, came_y, came_d, flops=US)
+    arrived = traded(terms, "yh")
     part = ((1, MODEL), F32)
     d_t, part_t = call(project_kernel, [col, part], cot_t, gt, wt_t, att_t, flops=2 * US)
     q_s, k_s, v_s = (swapped(x) for x in (qs, ks, vs))

time: 105 us -> 104 us (level)
  waiting for transfers between devices: 31.5 us -> 20.2 us
  starting transfers between devices: 55.1 us -> 65.4 us
    ppermute x5 -> x6, waiting for transfers between devices: 8.53 us -> 0.29 us  [partner(): return lax.ppermute(x, axis, [(0, 1), (1, 0)])]
    all_to_all x3, waiting for transfers between devices: 23 us -> 16 us  [traded(): return lax.all_to_all(x, axes, 0, 0, tiled=True)]
    all_to_all x3, starting transfers between devices: 39.5 us -> 43.7 us  [traded(): return lax.all_to_all(x, axes, 0, 0, tiled=True)]
    ppermute x0 -> x1, waiting for transfers between devices: none -> 3.88 us  [step(): came_d = lax.ppermute(to_d, ('xl', 'yl'), [(i, 3 - i) for i in range(4)])]
    ppermute x5 -> x6, starting transfers between devices: 15.5 us -> 18.8 us  [partner(): return lax.ppermute(x, axis, [(0, 1), (1, 0)])]
    ppermute x0 -> x1, starting transfers between devices: none -> 2.95 us  [step(): came_d = lax.ppermute(to_d, ('xl', 'yl'), [(i, 3 - i) for i in range(4)])]
  transfers between devices with their start and end apart: 8 -> 10, of which waited for: 6 -> 5; matrix products, arithmetic and copies ran while one was open for 2% -> 2% of each run, Pallas kernels for 11% -> 12%
where the time goes in v4:
time: 104 us; the launch traced here: 103 us
  starting transfers between devices  65.4 us (63%)
  waiting for transfers between devices  20.2 us (19%)
  Pallas kernels  13.6 us (13%)
  local copies, waits for them, and re-layouts  2.43 us (2%)
    all_to_all x3, starting transfers between devices, traded(): return lax.all_to_all(x, axes, 0, 0, tiled=True)  43.7 us
    ppermute x6, starting transfers between devices, partner(): return lax.ppermute(x, axis, [(0, 1), (1, 0)])  18.8 us
    all_to_all x3, waiting for transfers between devices, traded(): return lax.all_to_all(x, axes, 0, 0, tiled=True)  16 us
    pallas_call x11, Pallas kernels, call(): pl.pallas_call(kernel, out_shape=shapes, in_specs=specs, out_specs=tuple(...  13.6 us
    ppermute x1, waiting for transfers between devices, step(): came_d = lax.ppermute(to_d, ('xl', 'yl'), [(i, 3 - i) for i in range(4)])  3.88 us
    ppermute x1, starting transfers between devices, step(): came_d = lax.ppermute(to_d, ('xl', 'yl'), [(i, 3 - i) for i in range(4)])  2.95 us
    reshape x3, local copies, waits for them, and re-layouts, step(): q2, k2, v2 = (x.reshape(TOK, WIDTH) for x in (qt, kt, vt))  2.22 us
  transfers between devices with their start and end apart: 10, of which 5 were waited for; matrix products, arithmetic and copies ran while one was open for 2% of the time, Pallas kernels for 12%

profile of v4, /device:TPU:1, one launch (start us, length us, event | category | flops | bytes accessed | tf_op | source)
XLA Modules:
  0.0 103.2 jit_solution(11522691763497420490)
XLA Ops:
  0.6 0.0 copy-start.3
  0.7 23.4 %all-to-all-start = ((bf16[64,2,1152]{2,1,0:T(2,128)(2,1)}), bf16[64,2,1152]{2,1,0:T(2,128)(2,1)S(1)}, u32[]{:S(2)}, u32[]{:S(2)}) async-start(bf16[64,2,1152]{2,1,0:T(2,128)(2,1)} %bitcast.32), calls=%async_computation | async-start | bytes 589824 | tf_op jit(solution)/shard_map/all_to_all | solution.py:192
  24.1 2.4 %collective-permute-start.1 = (bf16[1,64,2,1152]{3,2,1,0:T(2,128)(2,1)}, bf16[1,64,2,1152]{3,2,1,0:T(2,128)(2,1)S(1)}, u32[]{:S(2)}, u32[]{:S(2)}) collective-permute-start(bf16[1,64,2,1152]{3,2,1,0:T(2,128)(2,1)} %param.11), channel_id=1, source_target_pairs={{0,1},{1,0},{2,3},{3,2},{4,5},{5,4},{6,7},{7,6},{8,9},{9,8},{10,11... | collective-permute-start | bytes 884744 | tf_op jit(solution)/shard_map/ppermute | solution.py:196
  26.4 1.0 %reshape.39.q_ref = bf16[128,576]{1,0:T(8,128)(2,1)S(1)} reshape(bf16[1,64,2,576]{3,2,1,0:T(2,128)(2,1)} %param.12) | data formatting | bytes 294912 | tf_op jit(solution)/shard_map/reshape | solution.py:220
  27.5 1.0 %reshape.40.k_ref = bf16[128,576]{1,0:T(8,128)(2,1)S(1)} reshape(bf16[1,64,2,576]{3,2,1,0:T(2,128)(2,1)} %param.13) | data formatting | bytes 294912 | tf_op jit(solution)/shard_map/reshape | solution.py:220
  28.5 0.0 copy-done.3
  28.5 0.1 reshape.41.v_ref
  28.7 0.0 copy-start
  28.7 0.0 copy-start.9
  28.7 1.0 %shard_map.178.att_ref.own_ref = bf16[576,128]{1,0:T(8,128)(2,1)S(1)} custom-call(bf16[128,576]{1,0:T(8,128)(2,1)S(1)} %reshape.39.q_ref, bf16[128,576]{1,0:T(8,128)(2,1)S(1)} %reshape.40.k_ref, bf16[128,576]{1,0:T(8,128)(2,1)S(1)} %reshape.41.v_ref), custom_call_target="tpu_custom_call" | custom-call | flops 1600000000 | bytes 1048576 | tf_op jit(solution)/shard_map/pallas_call | solution.py:180
  29.8 2.0 %collective-permute-start = (bf16[576,128]{1,0:T(8,128)(2,1)S(1)}, bf16[576,128]{1,0:T(8,128)(2,1)S(1)}, u32[]{:S(2)}, u32[]{:S(2)}) collective-permute-start(bf16[576,128]{1,0:T(8,128)(2,1)S(1)} %shard_map.178.att_ref.own_ref), channel_id=1, source_target_pairs={{0,1},{1,0},{2,3},{3,2},{4,5},{5,4},{6,7},{7,6},{8,9},{9,8},{10,11... | collective-permute-start | bytes 442376 | tf_op jit(solution)/shard_map/ppermute | solution.py:196
  31.7 0.0 collective-permute-done.1
  31.8 0.0 copy-done
  31.8 0.0 copy-done.9
  31.8 1.0 shard_map.184.sel_ref
  32.8 0.3 collective-permute-done.other_ref
  33.0 0.0 copy-start.4
  33.0 0.5 shard_map.185
  33.6 2.2 %collective-permute-start.2 = (bf16[4,162,128]{2,1,0:T(8,128)(2,1)S(1)}, bf16[4,162,128]{2,1,0:T(8,128)(2,1)S(1)}, u32[]{:S(2)}, u32[]{:S(2)}) collective-permute-start(bf16[4,162,128]{2,1,0:T(8,128)(2,1)S(1)} %get-tuple-element.34), channel_id=1, source_target_pairs={{0,512},{512,0},{1,513},{513,1},{2,514},{514,2},{3,515},{515,3},{4... | collective-permute-start | bytes 497672 | tf_op jit(solution)/shard_map/ppermute | solution.py:196
  35.8 3.2 %collective-permute-start.3 = (bf16[4,162,128]{2,1,0:T(8,128)(2,1)S(1)}, bf16[4,162,128]{2,1,0:T(8,128)(2,1)S(1)}, u32[]{:S(2)}, u32[]{:S(2)}) collective-permute-start(bf16[4,162,128]{2,1,0:T(8,128)(2,1)S(1)} %get-tuple-element.35), channel_id=1, source_target_pairs={{0,64},{64,0},{1,65},{65,1},{2,66},{66,2},{3,67},{67,3},{4,68},{68... | collective-permute-start | bytes 497672 | tf_op jit(solution)/shard_map/ppermute | solution.py:196
  39.0 2.9 %collective-permute-start.4 = (bf16[4,162,128]{2,1,0:T(8,128)(2,1)S(1)}, bf16[4,162,128]{2,1,0:T(8,128)(2,1)S(1)}, u32[]{:S(2)}, u32[]{:S(2)}) collective-permute-start(bf16[4,162,128]{2,1,0:T(8,128)(2,1)S(1)} %get-tuple-element.36), channel_id=1, source_target_pairs={{0,576},{64,512},{512,64},{576,0},{1,577},{65,513},{513,65},{577,1... | collective-permute-start | bytes 497672 | tf_op jit(solution)/shard_map/ppermute | solution.py:226
  42.0 0.0 copy-done.4
  42.0 0.0 copy-start.6
  42.0 0.0 copy-start.7
  42.0 0.0 copy-start.8
  42.0 0.9 shard_map.179
  42.9 0.0 copy-done.6
  42.9 0.1 copy-done.7
  43.0 0.1 copy-done.8
  43.0 0.9 shard_map.181.att_ref
  43.9 0.0 copy-start.5
  43.9 0.0 copy-start.10
  44.0 0.0 collective-permute-done.2.rest_0_
  44.0 0.0 collective-permute-done.3.rest_1_
  44.0 3.9 %collective-permute-done.4.rest_2_ = bf16[4,162,128]{2,1,0:T(8,128)(2,1)S(1)} collective-permute-done((bf16[4,162,128]{2,1,0:T(8,128)(2,1)S(1)}, bf16[4,162,128]{2,1,0:T(8,128)(2,1)S(1)}, u32[]{:S(2)}, u32[]{:S(2)}) %collective-permute-start.4) | collective-permute-done | bytes 165920 | tf_op jit(solution)/shard_map/ppermute | solution.py:226
  47.9 0.8 shard_map.186
  48.6 0.7 all-to-all-done.cot_ref
  49.3 6.8 %all-to-all-start.1 = ((bf16[4,162,128]{2,1,0:T(8,128)(2,1)}), bf16[4,162,128]{2,1,0:T(8,128)(2,1)S(1)}, u32[]{:S(2)}, u32[]{:S(2)}) async-start(bf16[4,162,128]{2,1,0:T(8,128)(2,1)} %shard_map.186), calls=%async_computation.1 | async-start | bytes 344064 | tf_op jit(solution)/shard_map/all_to_all | solution.py:192
  56.0 0.0 copy-done.5
  56.1 0.0 copy-done.10
  56.1 0.8 shard_map.182
  56.9 0.0 copy-start.1
  56.9 0.0 copy-start.2
  56.9 2.9 %collective-permute-start.5 = (f32[1,1152]{1,0:T(1,128)S(1)}, f32[1,1152]{1,0:T(1,128)S(1)}, u32[]{:S(2)}, u32[]{:S(2)}) collective-permute-start(f32[1,1152]{1,0:T(1,128)S(1)} %broadcast_select_fusion.2), channel_id=1, source_target_pairs={{0,1},{1,0},{2,3},{3,2},{4,5},{5,4},{6,7},{7,6},{8,9},{9,8},{10,11... | collective-permute-start | bytes 13832 | tf_op jit(solution)/shard_map/ppermute | solution.py:196
  59.8 3.9 %all-to-all-done.1.in_ref = bf16[4,162,128]{2,1,0:T(8,128)(2,1)S(1)} async-done(((bf16[4,162,128]{2,1,0:T(8,128)(2,1)}), bf16[4,162,128]{2,1,0:T(8,128)(2,1)S(1)}, u32[]{:S(2)}, u32[]{:S(2)}) %all-to-all-start.1) | async-done | bytes 165920 | tf_op jit(solution)/shard_map/all_to_all | solution.py:192
  63.7 0.0 collective-permute-done.5.came_ref
  63.7 0.8 shard_map.187
  64.5 13.5 %all-to-all-start.2 = ((bf16[32,16,128]{2,1,0:T(8,128)(2,1)}), bf16[32,16,128]{2,1,0:T(8,128)(2,1)S(1)}, u32[]{:S(2)}, u32[]{:S(2)}) async-start(bf16[32,16,128]{2,1,0:T(8,128)(2,1)} %shard_map.187), calls=%async_computation.2 | async-start | bytes 262144 | tf_op jit(solution)/shard_map/all_to_all | solution.py:192
  78.1 0.0 copy-done.1
  78.1 0.0 copy-done.2
  78.1 3.2 %shard_map.180 = (bf16[64,2,576]{2,1,0:T(2,128)(2,1)}, bf16[64,2,576]{2,1,0:T(2,128)(2,1)}, bf16[64,2,576]{2,1,0:T(2,128)(2,1)}) custom-call(bf16[64,2,576]{2,1,0:T(2,128)(2,1)S(1)} %bitcast.35, bf16[64,2,576]{2,1,0:T(2,128)(2,1)S(1)} %bitcast.36, bf16[64,2,576]{2,1,0:T(2,128)(2,1)S(1)} %bitcast.37, bf16[576,128]{1,0:T(8,128)(2,1)S(1)} %shard_map.178.att_ref.own_ref, ...), custom_call_target="tpu_custom_call" | custom-call | flops 1600000000 | bytes 1048576 | tf_op jit(solution)/shard_map/pallas_call | solution.py:180
  81.3 11.5 %all-to-all-done.2.in_ref = bf16[32,16,128]{2,1,0:T(8,128)(2,1)S(1)} async-done(((bf16[32,16,128]{2,1,0:T(8,128)(2,1)}), bf16[32,16,128]{2,1,0:T(8,128)(2,1)S(1)}, u32[]{:S(2)}, u32[]{:S(2)}) %all-to-all-start.2) | async-done | bytes 131104 | tf_op jit(solution)/shard_map/all_to_all | solution.py:192
  92.8 0.8 shard_map.188
  93.6 6.1 %collective-permute-start.6 = (f32[1,1152]{1,0:T(1,128)S(1)}, f32[1,1152]{1,0:T(1,128)S(1)}, u32[]{:S(2)}, u32[]{:S(2)}) collective-permute-start(f32[1,1152]{1,0:T(1,128)S(1)} %get-tuple-element.40), channel_id=1, source_target_pairs={{0,1},{1,0},{2,3},{3,2},{4,5},{5,4},{6,7},{7,6},{8,9},{9,8},{10,11... | collective-permute-start | bytes 13832 | tf_op jit(solution)/shard_map/ppermute | solution.py:196
  99.7 2.9 %shard_map.183 = (bf16[576,128]{1,0:T(8,128)(2,1)}, bf16[576,128]{1,0:T(8,128)(2,1)}, bf16[576,128]{1,0:T(8,128)(2,1)}) custom-call(bf16[576,128]{1,0:T(8,128)(2,1)S(1)} %bitcast.42, bf16[576,128]{1,0:T(8,128)(2,1)S(1)} %bitcast.44, bf16[576,128]{1,0:T(8,128)(2,1)S(1)} %bitcast.46, bf16[576,128]{1,0:T(8,128)(2,1)S(1)} %shard_map.181.att_ref, ...), custom_call_target="tpu_custom_call" | custom-call | flops 1600000000 | bytes 1048576 | tf_op jit(solution)/shard_map/pallas_call | solution.py:180
  102.6 0.0 collective-permute-done.6
  102.6 0.6 broadcast_select_fusion
  (1 shorter events, 0.0 us)
Async XLA Ops:
  0.6 27.9 %copy-start.3 = (bf16[1,64,2,576]{3,2,1,0:T(2,128)(2,1)S(1)}, bf16[1,64,2,576]{3,2,1,0:T(2,128)(2,1)}, u32[]{:S(2)}) copy-start(bf16[1,64,2,576]{3,2,1,0:T(2,128)(2,1)} %param.14) | copy-start | bytes 442372
  0.7 48.6 %all-to-all-start = ((bf16[64,2,1152]{2,1,0:T(2,128)(2,1)}), bf16[64,2,1152]{2,1,0:T(2,128)(2,1)S(1)}, u32[]{:S(2)}, u32[]{:S(2)}) async-start(bf16[64,2,1152]{2,1,0:T(2,128)(2,1)} %bitcast.32), calls=%async_computation | async-start | bytes 589824 | tf_op jit(solution)/shard_map/all_to_all | solution.py:192
  24.1 7.7 %collective-permute-start.1 = (bf16[1,64,2,1152]{3,2,1,0:T(2,128)(2,1)}, bf16[1,64,2,1152]{3,2,1,0:T(2,128)(2,1)S(1)}, u32[]{:S(2)}, u32[]{:S(2)}) collective-permute-start(bf16[1,64,2,1152]{3,2,1,0:T(2,128)(2,1)} %param.11), channel_id=1, source_target_pairs={{0,1},{1,0},{2,3},{3,2},{4,5},{5,4},{6,7},{7,6},{8,9},{9,8},{10,11... | collective-permute-start | bytes 884744 | tf_op jit(solution)/shard_map/ppermute | solution.py:196
  28.7 3.1 %copy-start = (bf16[1,64,2,1152]{3,2,1,0:T(2,128)(2,1)S(1)}, bf16[1,64,2,1152]{3,2,1,0:T(2,128)(2,1)}, u32[]{:S(2)}) copy-start(bf16[1,64,2,1152]{3,2,1,0:T(2,128)(2,1)} %param.11) | copy-start | bytes 884740
  28.7 3.1 %copy-start.9 = (f32[1,1152]{1,0:T(1,128)S(1)}, f32[1,1152]{1,0:T(1,128)}, u32[]{:S(2)}) copy-start(f32[1,1152]{1,0:T(1,128)} %gate_ref.5) | copy-start | bytes 13828
  29.8 3.3 %collective-permute-start = (bf16[576,128]{1,0:T(8,128)(2,1)S(1)}, bf16[576,128]{1,0:T(8,128)(2,1)S(1)}, u32[]{:S(2)}, u32[]{:S(2)}) collective-permute-start(bf16[576,128]{1,0:T(8,128)(2,1)S(1)} %shard_map.178.att_ref.own_ref), channel_id=1, source_target_pairs={{0,1},{1,0},{2,3},{3,2},{4,5},{5,4},{6,7},{7,6},{8,9},{9,8},{10,11... | collective-permute-start | bytes 442376 | tf_op jit(solution)/shard_map/ppermute | solution.py:196
  33.0 8.9 %copy-start.4 = (bf16[1152,576]{0,1:T(8,128)(2,1)S(1)}, bf16[1152,576]{0,1:T(8,128)(2,1)}, u32[]{:S(2)}) copy-start(bf16[1152,576]{0,1:T(8,128)(2,1)} %param.18) | copy-start | bytes 3981316
  33.6 10.4 %collective-permute-start.2 = (bf16[4,162,128]{2,1,0:T(8,128)(2,1)S(1)}, bf16[4,162,128]{2,1,0:T(8,128)(2,1)S(1)}, u32[]{:S(2)}, u32[]{:S(2)}) collective-permute-start(bf16[4,162,128]{2,1,0:T(8,128)(2,1)S(1)} %get-tuple-element.34), channel_id=1, source_target_pairs={{0,512},{512,0},{1,513},{513,1},{2,514},{514,2},{3,515},{515,3},{4... | collective-permute-start | bytes 497672 | tf_op jit(solution)/shard_map/ppermute | solution.py:196
  35.8 8.2 %collective-permute-start.3 = (bf16[4,162,128]{2,1,0:T(8,128)(2,1)S(1)}, bf16[4,162,128]{2,1,0:T(8,128)(2,1)S(1)}, u32[]{:S(2)}, u32[]{:S(2)}) collective-permute-start(bf16[4,162,128]{2,1,0:T(8,128)(2,1)S(1)} %get-tuple-element.35), channel_id=1, source_target_pairs={{0,64},{64,0},{1,65},{65,1},{2,66},{66,2},{3,67},{67,3},{4,68},{68... | collective-permute-start | bytes 497672 | tf_op jit(solution)/shard_map/ppermute | solution.py:196
  39.0 8.9 %collective-permute-start.4 = (bf16[4,162,128]{2,1,0:T(8,128)(2,1)S(1)}, bf16[4,162,128]{2,1,0:T(8,128)(2,1)S(1)}, u32[]{:S(2)}, u32[]{:S(2)}) collective-permute-start(bf16[4,162,128]{2,1,0:T(8,128)(2,1)S(1)} %get-tuple-element.36), channel_id=1, source_target_pairs={{0,576},{64,512},{512,64},{576,0},{1,577},{65,513},{513,65},{577,1... | collective-permute-start | bytes 497672 | tf_op jit(solution)/shard_map/ppermute | solution.py:226
  42.0 0.9 copy-start.6
  42.0 1.0 copy-start.7
  42.0 1.0 %copy-start.8 = (bf16[1,1,128,576]{2,3,1,0:T(8,128)(2,1)S(1)}, bf16[1,1,128,576]{2,3,1,0:T(8,128)(2,1)}, u32[]{:S(2)}) copy-start(bf16[1,1,128,576]{2,3,1,0:T(8,128)(2,1)} %param.17) | copy-start | bytes 442372
  43.9 12.1 %copy-start.5 = (bf16[1152,576]{0,1:T(8,128)(2,1)S(1)}, bf16[1152,576]{0,1:T(8,128)(2,1)}, u32[]{:S(2)}) copy-start(bf16[1152,576]{0,1:T(8,128)(2,1)} %param.19) | copy-start | bytes 3981316
  43.9 12.1 %copy-start.10 = (f32[1,1152]{1,0:T(1,128)S(1)}, f32[1,1152]{1,0:T(1,128)}, u32[]{:S(2)}) copy-start(f32[1,1152]{1,0:T(1,128)} %gate_ref.4) | copy-start | bytes 13828
  49.3 14.4 %all-to-all-start.1 = ((bf16[4,162,128]{2,1,0:T(8,128)(2,1)}), bf16[4,162,128]{2,1,0:T(8,128)(2,1)S(1)}, u32[]{:S(2)}, u32[]{:S(2)}) async-start(bf16[4,162,128]{2,1,0:T(8,128)(2,1)} %shard_map.186), calls=%async_computation.1 | async-start | bytes 344064 | tf_op jit(solution)/shard_map/all_to_all | solution.py:192
  56.9 21.2 %copy-start.1 = (bf16[1,64,2,576]{3,2,1,0:T(2,128)(2,1)S(1)}, bf16[1,64,2,576]{3,2,1,0:T(2,128)(2,1)}, u32[]{:S(2)}) copy-start(bf16[1,64,2,576]{3,2,1,0:T(2,128)(2,1)} %param.12) | copy-start | bytes 442372
  56.9 21.2 %copy-start.2 = (bf16[1,64,2,576]{3,2,1,0:T(2,128)(2,1)S(1)}, bf16[1,64,2,576]{3,2,1,0:T(2,128)(2,1)}, u32[]{:S(2)}) copy-start(bf16[1,64,2,576]{3,2,1,0:T(2,128)(2,1)} %param.13) | copy-start | bytes 442372
  56.9 6.7 %collective-permute-start.5 = (f32[1,1152]{1,0:T(1,128)S(1)}, f32[1,1152]{1,0:T(1,128)S(1)}, u32[]{:S(2)}, u32[]{:S(2)}) collective-permute-start(f32[1,1152]{1,0:T(1,128)S(1)} %broadcast_select_fusion.2), channel_id=1, source_target_pairs={{0,1},{1,0},{2,3},{3,2},{4,5},{5,4},{6,7},{7,6},{8,9},{9,8},{10,11... | collective-permute-start | bytes 13832 | tf_op jit(solution)/shard_map/ppermute | solution.py:196
  64.5 28.3 %all-to-all-start.2 = ((bf16[32,16,128]{2,1,0:T(8,128)(2,1)}), bf16[32,16,128]{2,1,0:T(8,128)(2,1)S(1)}, u32[]{:S(2)}, u32[]{:S(2)}) async-start(bf16[32,16,128]{2,1,0:T(8,128)(2,1)} %shard_map.187), calls=%async_computation.2 | async-start | bytes 262144 | tf_op jit(solution)/shard_map/all_to_all | solution.py:192
  93.6 9.0 %collective-permute-start.6 = (f32[1,1152]{1,0:T(1,128)S(1)}, f32[1,1152]{1,0:T(1,128)S(1)}, u32[]{:S(2)}, u32[]{:S(2)}) collective-permute-start(f32[1,1152]{1,0:T(1,128)S(1)} %get-tuple-element.40), channel_id=1, source_target_pairs={{0,1},{1,0},{2,3},{3,2},{4,5},{5,4},{6,7},{7,6},{8,9},{9,8},{10,11... | collective-permute-start | bytes 13832 | tf_op jit(solution)/shard_map/ppermute | solution.py:196
